TPU v7x, 128 devices: a whole 4x4x4 slice. The times are simulated.
128 devices in a mesh: seq: 64 (over z, y_lo, x, core), head: 2 (over y_hi).
Axes of the slice: x: 4, y: 4 (y_hi: 2, y_lo: 2; y = y_hi * 2 + y_lo), z: 4, core: 2. Of those that a mesh axis runs over, the one named last changes fastest.
Arguments:
- tokens: bfloat16 [32768, 4096], P('seq'), may hold values from -18 to 18
- norm_gain: float32 [4096], replicated, may hold values from 0.5 to 1.5
- w_query: bfloat16 [4096, 2048], P(None, 'head'), may hold values from -0.0625 to 0.0625
- w_key: bfloat16 [4096, 512], P(None, 'head'), may hold values from -1.90625 to 1.90625
- w_value: bfloat16 [4096, 512], P(None, 'head'), may hold values from -0.09375 to 0.09375
- w_out: bfloat16 [2048, 4096], P('head'), may hold values from -0.125 to 0.125
- window: int32 [16], P('head'), may hold values from 256 to 4096, as said below
- sink_count: int32 [16], P('head'), may hold values from 1 to 4, as said below
- sink_bias: float32 [16], P('head'), may hold values from 4 to 8
Outputs:
- mixed: bfloat16 [32768, 4096], P('seq', 'head')
Inputs may be any that keep to these rules, and one draw needn't show every extreme that they name: Some head's window is exactly 4096. `sink_count`: some head's count is exactly 4.
All inputs are finite; a program needn't handle non-finite values.
Results may differ from a plain program's by a relative error of at most 0.0071.
Values may be sent and summed in bfloat16 or wider, within the bound.
A program may use at most 128 MiB of HBM per device.

v0:
```python
import jax
import jax.numpy as jnp
from jax import lax
from jax.sharding import PartitionSpec as P

HEAD_DIM = 128
SINK = 4
SPAN = 9


EPSILON = 1e-05


def picked(shard, axis, root):
    return lax.dynamic_index_in_dim(lax.all_gather(shard, axis), root, 0, keepdims=False)


def shifted(shard, axis, by):
    peers = lax.axis_size(axis)
    pairs = [(i, i + by) for i in range(peers) if 0 <= i + by < peers]
    return lax.ppermute(shard, axis, pairs)


def split_up(shard, dim, peers):
    lengths = shard.shape
    parts = shard.reshape(*lengths[:dim], peers, lengths[dim] // peers, *lengths[dim + 1 :])
    return jnp.moveaxis(parts, dim, 0)


def sent_and_summed(shard, axis, dim):
    parts = split_up(shard, dim, lax.axis_size(axis))
    arrived = lax.all_to_all(parts, axis, split_axis=0, concat_axis=0, tiled=True)
    return arrived.astype(jnp.float32).sum(axis=0)


def normalize(tokens, norm_gain):
    widened = tokens.astype(jnp.float32)
    row_scale = lax.rsqrt(jnp.mean(widened * widened, axis=1, keepdims=True) + EPSILON)
    return (widened, (widened * row_scale * norm_gain).astype(jnp.bfloat16))


def attend(
    queries,
    block_keys,
    block_values,
    anchor_key_rows,
    anchor_value_rows,
    query_start,
    key_start,
    window,
    sink_count,
    sink_bias,
):
    tok_rows, heads_here, head_width = queries.shape
    key_rows, groups_here, _ = block_keys.shape
    per_group = heads_here // groups_here
    softmax_scale = head_width ** (-0.5)
    query_pos = (query_start + jnp.arange(tok_rows, dtype=jnp.int32))[:, None]
    key_pos = (key_start + jnp.arange(key_rows, dtype=jnp.int32))[None, :]
    sink_pos = jnp.arange(anchor_key_rows.shape[0], dtype=jnp.int32)[None, :]

    def one_head(index):
        group = index // per_group
        head_queries = lax.dynamic_index_in_dim(queries, index, 1, keepdims=False)
        head_keys = lax.dynamic_index_in_dim(block_keys, group, 1, keepdims=False)
        head_values = lax.dynamic_index_in_dim(block_values, group, 1, keepdims=False)
        head_sink_keys = lax.dynamic_index_in_dim(anchor_key_rows, group, 1, keepdims=False)
        head_sink_values = lax.dynamic_index_in_dim(anchor_value_rows, group, 1, keepdims=False)
        reach_rows = window[index]
        open_sinks = sink_count[index]
        scores = (
            jnp.einsum("te,le->tl", head_queries, head_keys, preferred_element_type=jnp.float32)
            * softmax_scale
        )
        anchor_score_rows = (
            jnp.einsum(
                "te,se->ts", head_queries, head_sink_keys, preferred_element_type=jnp.float32
            )
            * softmax_scale
        )
        anchor_score_rows = anchor_score_rows + sink_bias[index]
        visible = (key_pos <= query_pos) & (key_pos > query_pos - reach_rows) & (key_pos >= 0)
        sink_open = (sink_pos < open_sinks) & (sink_pos <= query_pos - reach_rows)
        scores = jnp.where(visible, scores, -1e30)
        anchor_score_rows = jnp.where(sink_open, anchor_score_rows, -1e30)
        peak_score = jnp.maximum(
            jnp.max(scores, axis=1, keepdims=True),
            jnp.max(anchor_score_rows, axis=1, keepdims=True),
        )
        weights = jnp.exp(scores - peak_score)
        anchor_weight_rows = jnp.exp(anchor_score_rows - peak_score)
        denominator = jnp.sum(weights, axis=1, keepdims=True) + jnp.sum(
            anchor_weight_rows, axis=1, keepdims=True
        )
        weights = (weights / denominator).astype(jnp.bfloat16)
        anchor_weight_rows = (anchor_weight_rows / denominator).astype(jnp.bfloat16)
        merged_scores = jnp.einsum(
            "tl,le->te", weights, head_values, preferred_element_type=jnp.float32
        )
        merged_scores = merged_scores + jnp.einsum(
            "ts,se->te", anchor_weight_rows, head_sink_values, preferred_element_type=jnp.float32
        )
        return merged_scores.astype(jnp.bfloat16)

    per_head = lax.map(one_head, jnp.arange(heads_here, dtype=jnp.int32))
    return jnp.transpose(per_head, (1, 0, 2)).reshape(tok_rows, heads_here * head_width)


def local(tokens, norm_gain, w_query, w_key, w_value, w_out, window, sink_count, sink_bias):
    widened, normed = normalize(tokens, norm_gain)
    tok_rows = tokens.shape[0]
    heads_here = w_query.shape[1] // HEAD_DIM
    groups_here = w_key.shape[1] // HEAD_DIM
    queries = (
        jnp.dot(normed, w_query, preferred_element_type=jnp.float32)
        .astype(jnp.bfloat16)
        .reshape(tok_rows, heads_here, HEAD_DIM)
    )
    key_value = jnp.stack(
        [
            jnp.dot(normed, w_key, preferred_element_type=jnp.float32).astype(jnp.bfloat16),
            jnp.dot(normed, w_value, preferred_element_type=jnp.float32).astype(jnp.bfloat16),
        ]
    )
    sink_rows = picked(normed[:SINK], "seq", 0)
    sink_pair = jnp.stack(
        [
            jnp.dot(sink_rows, w_key, preferred_element_type=jnp.float32).astype(jnp.bfloat16),
            jnp.dot(sink_rows, w_value, preferred_element_type=jnp.float32).astype(jnp.bfloat16),
        ]
    )
    buffer = jnp.zeros((2, SPAN * tok_rows, key_value.shape[2]), jnp.bfloat16)
    buffer = lax.dynamic_update_slice_in_dim(buffer, key_value, (SPAN - 1) * tok_rows, 1)

    def advance(offset, loop_state):
        gathered, moving = loop_state
        moving = shifted(moving, "seq", 1)
        gathered = lax.dynamic_update_slice_in_dim(
            gathered, moving, (SPAN - 2 - offset) * tok_rows, 1
        )
        return (gathered, moving)

    buffer, _ = lax.fori_loop(0, SPAN - 1, advance, (buffer, key_value))
    block_index = lax.axis_index("seq")
    query_start = block_index * tok_rows
    key_start = query_start - (SPAN - 1) * tok_rows
    key_rows = SPAN * tok_rows
    attended = attend(
        queries,
        buffer[0].reshape(key_rows, groups_here, HEAD_DIM),
        buffer[1].reshape(key_rows, groups_here, HEAD_DIM),
        sink_pair[0].reshape(SINK, groups_here, HEAD_DIM),
        sink_pair[1].reshape(SINK, groups_here, HEAD_DIM),
        query_start,
        key_start,
        window,
        sink_count,
        sink_bias,
    )
    partial_value = (
        jnp.dot(attended, w_out, preferred_element_type=jnp.float32)
        .astype(jnp.bfloat16)
        .astype(jnp.float32)
    )
    summed = sent_and_summed(partial_value.astype(jnp.bfloat16), "head", 1)
    share_width = summed.shape[1]
    residual = lax.dynamic_slice_in_dim(
        widened, lax.axis_index("head") * share_width, share_width, 1
    )
    return (residual + summed).astype(jnp.bfloat16)


def solution(mesh):
    in_specs = (
        P("seq", None),
        P(),
        P(None, "head"),
        P(None, "head"),
        P(None, "head"),
        P("head", None),
        P("head"),
        P("head"),
        P("head"),
    )
    out_specs = P("seq", "head")
    return jax.shard_map(local, mesh=mesh, in_specs=in_specs, out_specs=out_specs, check_vma=False)
```

profile of v0, /device:TPU:96, one launch (start us, length us, event | category | flops | bytes accessed | tf_op | source)
XLA Modules:
  0.0 370.6 jit_solution(353741818888850092)
XLA Ops:
  23.2 115.9 %while.29 = (s32[]{:T(128)}, bf16[2,4608,256]{2,1,0:T(8,128)(2,1)}, bf16[2,512,256]{2,1,0:T(8,128)(2,1)S(1)}, s32[]{:T(128)}, s32[]{:T(128)}, /*index=5*/s32[]{:T(128)}, s32[]{:T(128)}, s32[]{:T(128)}) while((s32[]{:T(128)}, bf16[2,4608,256]{2,1,0:T(8,128)(2,1)}, bf16[2,512,256]{2,1,0:T(8,128)(2,1)S(1)}, s32[]{:T(128)}, s32[]{:T(128)}, ...), condition=%wide.region_2.3_spmd, body=%wide.region_1.2_spmd.sunk | while | flops 7 | bytes 4194491 | solution.py:143
  25.1 11.7 %collective-permute-done = bf16[2,512,256]{2,1,0:T(8,128)(2,1)S(1)} collective-permute-done((bf16[2,512,256]{2,1,0:T(8,128)(2,1)S(1)}, bf16[2,512,256]{2,1,0:T(8,128)(2,1)S(1)}, u32[]{:S(2)}, u32[]{:S(2)}) %collective-permute-start) | collective-permute-done | bytes 524320 | tf_op jit(solution)/shard_map/while/body/eval_jaxpr/ppermute | solution.py:21
  39.6 11.7 %collective-permute-done = bf16[2,512,256]{2,1,0:T(8,128)(2,1)S(1)} collective-permute-done((bf16[2,512,256]{2,1,0:T(8,128)(2,1)S(1)}, bf16[2,512,256]{2,1,0:T(8,128)(2,1)S(1)}, u32[]{:S(2)}, u32[]{:S(2)}) %collective-permute-start) | collective-permute-done | bytes 524320 | tf_op jit(solution)/shard_map/while/body/eval_jaxpr/ppermute | solution.py:21
  54.0 11.7 %collective-permute-done = bf16[2,512,256]{2,1,0:T(8,128)(2,1)S(1)} collective-permute-done((bf16[2,512,256]{2,1,0:T(8,128)(2,1)S(1)}, bf16[2,512,256]{2,1,0:T(8,128)(2,1)S(1)}, u32[]{:S(2)}, u32[]{:S(2)}) %collective-permute-start) | collective-permute-done | bytes 524320 | tf_op jit(solution)/shard_map/while/body/eval_jaxpr/ppermute | solution.py:21
  68.5 11.7 %collective-permute-done = bf16[2,512,256]{2,1,0:T(8,128)(2,1)S(1)} collective-permute-done((bf16[2,512,256]{2,1,0:T(8,128)(2,1)S(1)}, bf16[2,512,256]{2,1,0:T(8,128)(2,1)S(1)}, u32[]{:S(2)}, u32[]{:S(2)}) %collective-permute-start) | collective-permute-done | bytes 524320 | tf_op jit(solution)/shard_map/while/body/eval_jaxpr/ppermute | solution.py:21
  83.0 11.7 %collective-permute-done = bf16[2,512,256]{2,1,0:T(8,128)(2,1)S(1)} collective-permute-done((bf16[2,512,256]{2,1,0:T(8,128)(2,1)S(1)}, bf16[2,512,256]{2,1,0:T(8,128)(2,1)S(1)}, u32[]{:S(2)}, u32[]{:S(2)}) %collective-permute-start) | collective-permute-done | bytes 524320 | tf_op jit(solution)/shard_map/while/body/eval_jaxpr/ppermute | solution.py:21
  97.5 11.7 %collective-permute-done = bf16[2,512,256]{2,1,0:T(8,128)(2,1)S(1)} collective-permute-done((bf16[2,512,256]{2,1,0:T(8,128)(2,1)S(1)}, bf16[2,512,256]{2,1,0:T(8,128)(2,1)S(1)}, u32[]{:S(2)}, u32[]{:S(2)}) %collective-permute-start) | collective-permute-done | bytes 524320 | tf_op jit(solution)/shard_map/while/body/eval_jaxpr/ppermute | solution.py:21
  112.0 11.7 %collective-permute-done = bf16[2,512,256]{2,1,0:T(8,128)(2,1)S(1)} collective-permute-done((bf16[2,512,256]{2,1,0:T(8,128)(2,1)S(1)}, bf16[2,512,256]{2,1,0:T(8,128)(2,1)S(1)}, u32[]{:S(2)}, u32[]{:S(2)}) %collective-permute-start) | collective-permute-done | bytes 524320 | tf_op jit(solution)/shard_map/while/body/eval_jaxpr/ppermute | solution.py:21
  126.5 11.7 %collective-permute-done = bf16[2,512,256]{2,1,0:T(8,128)(2,1)S(1)} collective-permute-done((bf16[2,512,256]{2,1,0:T(8,128)(2,1)S(1)}, bf16[2,512,256]{2,1,0:T(8,128)(2,1)S(1)}, u32[]{:S(2)}, u32[]{:S(2)}) %collective-permute-start) | collective-permute-done | bytes 524320 | tf_op jit(solution)/shard_map/while/body/eval_jaxpr/ppermute | solution.py:21
  139.0 6.7 %copy.22 = bf16[2,4608,256]{1,2,0:T(8,128)(2,1)} copy(bf16[2,4608,256]{2,1,0:T(8,128)(2,1)} %get-tuple-element.246) | data formatting | bytes 9437184 | tf_op jit(solution)/shard_map/while | solution.py:143
  145.8 9.1 %fusion.31 = bf16[64,8,8,128]{3,2,1,0:T(8,128)(2,1)S(1)} fusion(bf16[512,4096]{1,0:T(8,128)(2,1)} %copy-done.4, bf16[4096,1024]{1,0:T(8,128)(2,1)} %param.15), kind=kOutput, calls=%fused_computation.50 | convolution fusion | flops 4295491584 | bytes 13631488 | tf_op jit(solution)/shard_map/dot_general | solution.py:115
  155.1 4.8 %fusion.38 = (bf16[1,4608,256]{1,2,0:T(8,128)(2,1)}, bf16[1,4608,256]{1,2,0:T(8,128)(2,1)}) fusion(bf16[2,4608,256]{1,2,0:T(8,128)(2,1)} %copy.22), kind=kLoop, calls=%fused_computation.66 | loop fusion | bytes 9437184 | tf_op jit(solution)/shard_map/slice | solution.py:151
  163.2 138.2 %while.30 = (s32[]{:T(128)}, bf16[8,512,128]{1,2,0:T(8,128)(2,1)}, s32[8]{0:T(128)S(1)}, s32[8]{0:T(128)S(1)}, bf16[512,8,128]{2,0,1:T(8,128)(2,1)S(1)}, /*index...) while((s32[]{:T(128)}, bf16[8,512,128]{1,2,0:T(8,128)(2,1)}, ...), condition=%wide.region_8.9_spmd.clone.clone, body=%wide.region_3.8_spmd.clone.clone.sunk | while | flops 1237482496 | bytes 41690104 | solution.py:105
  169.0 4.5 %fusion.59 = (f32[512]{0:T(512)S(1)}, f32[512,4608]{1,0:T(8,128)S(1)}) fusion(bf16[4608,2,128]{0,2,1:T(8,128)(2,1)} %get-tuple-element.562, s32[]{:T(128)S(6)} %select_n.74, bf16[512,8,128]{2,0,1:T(8,128)(2,1)S(1)} %get-tuple-element.561, s32[]{:T(128)S(6)} %select_n.75, pred[4608]{0:T(1024)(128)(4,1)S(1)} %broadcast_compare_fusion.2, ...), kind=kOutput, calls=%fused_computation.64.clone.1 | convolution fusion | flops 620494336 | bytes 10779656 | tf_op jit(solution)/shard_map/while/body/eval_jaxpr/te,le->tl/dot_general | solution.py:72
  186.2 4.4 %fusion.59 = (f32[512]{0:T(512)S(1)}, f32[512,4608]{1,0:T(8,128)S(1)}) fusion(bf16[4608,2,128]{0,2,1:T(8,128)(2,1)} %get-tuple-element.562, s32[]{:T(128)S(6)} %select_n.74, bf16[512,8,128]{2,0,1:T(8,128)(2,1)S(1)} %get-tuple-element.561, s32[]{:T(128)S(6)} %select_n.75, pred[4608]{0:T(1024)(128)(4,1)S(1)} %broadcast_compare_fusion.2, ...), kind=kOutput, calls=%fused_computation.64.clone.1 | convolution fusion | flops 620494336 | bytes 10779656 | tf_op jit(solution)/shard_map/while/body/eval_jaxpr/te,le->tl/dot_general | solution.py:72
  220.8 4.4 %fusion.59 = (f32[512]{0:T(512)S(1)}, f32[512,4608]{1,0:T(8,128)S(1)}) fusion(bf16[4608,2,128]{0,2,1:T(8,128)(2,1)} %get-tuple-element.562, s32[]{:T(128)S(6)} %select_n.74, bf16[512,8,128]{2,0,1:T(8,128)(2,1)S(1)} %get-tuple-element.561, s32[]{:T(128)S(6)} %select_n.75, pred[4608]{0:T(1024)(128)(4,1)S(1)} %broadcast_compare_fusion.2, ...), kind=kOutput, calls=%fused_computation.64.clone.1 | convolution fusion | flops 620494336 | bytes 10779656 | tf_op jit(solution)/shard_map/while/body/eval_jaxpr/te,le->tl/dot_general | solution.py:72
  238.1 4.4 %fusion.59 = (f32[512]{0:T(512)S(1)}, f32[512,4608]{1,0:T(8,128)S(1)}) fusion(bf16[4608,2,128]{0,2,1:T(8,128)(2,1)} %get-tuple-element.562, s32[]{:T(128)S(6)} %select_n.74, bf16[512,8,128]{2,0,1:T(8,128)(2,1)S(1)} %get-tuple-element.561, s32[]{:T(128)S(6)} %select_n.75, pred[4608]{0:T(1024)(128)(4,1)S(1)} %broadcast_compare_fusion.2, ...), kind=kOutput, calls=%fused_computation.64.clone.1 | convolution fusion | flops 620494336 | bytes 10779656 | tf_op jit(solution)/shard_map/while/body/eval_jaxpr/te,le->tl/dot_general | solution.py:72
  255.3 4.4 %fusion.59 = (f32[512]{0:T(512)S(1)}, f32[512,4608]{1,0:T(8,128)S(1)}) fusion(bf16[4608,2,128]{0,2,1:T(8,128)(2,1)} %get-tuple-element.562, s32[]{:T(128)S(6)} %select_n.74, bf16[512,8,128]{2,0,1:T(8,128)(2,1)S(1)} %get-tuple-element.561, s32[]{:T(128)S(6)} %select_n.75, pred[4608]{0:T(1024)(128)(4,1)S(1)} %broadcast_compare_fusion.2, ...), kind=kOutput, calls=%fused_computation.64.clone.1 | convolution fusion | flops 620494336 | bytes 10779656 | tf_op jit(solution)/shard_map/while/body/eval_jaxpr/te,le->tl/dot_general | solution.py:72
  272.6 4.4 %fusion.59 = (f32[512]{0:T(512)S(1)}, f32[512,4608]{1,0:T(8,128)S(1)}) fusion(bf16[4608,2,128]{0,2,1:T(8,128)(2,1)} %get-tuple-element.562, s32[]{:T(128)S(6)} %select_n.74, bf16[512,8,128]{2,0,1:T(8,128)(2,1)S(1)} %get-tuple-element.561, s32[]{:T(128)S(6)} %select_n.75, pred[4608]{0:T(1024)(128)(4,1)S(1)} %broadcast_compare_fusion.2, ...), kind=kOutput, calls=%fused_computation.64.clone.1 | convolution fusion | flops 620494336 | bytes 10779656 | tf_op jit(solution)/shard_map/while/body/eval_jaxpr/te,le->tl/dot_general | solution.py:72
  289.9 4.4 %fusion.59 = (f32[512]{0:T(512)S(1)}, f32[512,4608]{1,0:T(8,128)S(1)}) fusion(bf16[4608,2,128]{0,2,1:T(8,128)(2,1)} %get-tuple-element.562, s32[]{:T(128)S(6)} %select_n.74, bf16[512,8,128]{2,0,1:T(8,128)(2,1)S(1)} %get-tuple-element.561, s32[]{:T(128)S(6)} %select_n.75, pred[4608]{0:T(1024)(128)(4,1)S(1)} %broadcast_compare_fusion.2, ...), kind=kOutput, calls=%fused_computation.64.clone.1 | convolution fusion | flops 620494336 | bytes 10779656 | tf_op jit(solution)/shard_map/while/body/eval_jaxpr/te,le->tl/dot_general | solution.py:72
  301.4 8.3 %convolution_convert_fusion = bf16[512,4096]{1,0:T(8,128)(2,1)S(1)} fusion(bf16[512,1024]{0,1:T(8,128)(2,1)} %bitcast.106, bf16[1024,4096]{1,0:T(8,128)(2,1)} %param.18), kind=kOutput, calls=%fused_computation.46 | convolution fusion | flops 4297064448 | bytes 13631488 | tf_op jit(solution)/shard_map/dot_general | solution.py:161
  311.9 5.6 %all-to-all-start = ((bf16[2,512,2048]{2,1,0:T(8,128)(2,1)}), bf16[2,512,2048]{2,1,0:T(8,128)(2,1)}, u32[]{:S(2)}, u32[]{:S(2)}) async-start(bf16[2,512,2048]{2,1,0:T(8,128)(2,1)} %bitcast.99), calls=%async_computation | async-start | bytes 8388608 | tf_op jit(solution)/shard_map/all_to_all | solution.py:32
  317.6 6.5 %convert_element_type.50 = f32[512,4096]{1,0:T(8,128)} convert(bf16[512,4096]{1,0:T(8,128)(2,1)} %param.13) | non-fusion elementwise | flops 2097152 | bytes 12582912 | tf_op jit(solution)/shard_map/convert_element_type | solution.py:37
  324.1 33.1 %all-to-all-done = bf16[2,512,2048]{2,1,0:T(8,128)(2,1)} async-done(((bf16[2,512,2048]{2,1,0:T(8,128)(2,1)}), bf16[2,512,2048]{2,1,0:T(8,128)(2,1)}, u32[]{:S(2)}, u32[]{:S(2)}) %all-to-all-start) | async-done | bytes 4194336 | tf_op jit(solution)/shard_map/all_to_all | solution.py:32
  (224 shorter events, 126.9 us)
Async XLA Ops:
  6.5 8.7 %copy-start = (bf16[4096,256]{1,0:T(8,128)(2,1)S(1)}, bf16[4096,256]{1,0:T(8,128)(2,1)}, u32[]{:S(2)}) copy-start(bf16[4096,256]{1,0:T(8,128)(2,1)} %param.16) | copy-start | bytes 6291460
  6.5 153.4 %all-gather.4.cloned.1.call-start = ((), (), s32[]{:S(2)}) async-start(), calls=%async_computation.1 | async-start | bytes 2129920 | tf_op jit(solution)/shard_map/all_gather | solution.py:15
  6.5 3.6 copy-start.2
  12.5 2.1 copy-start.4
  15.2 3.6 copy-start.5
  15.2 4.1 %copy-start.7 = (bf16[4096,256]{1,0:T(8,128)(2,1)S(1)}, bf16[4096,256]{1,0:T(8,128)(2,1)}, u32[]{:S(2)}) copy-start(bf16[4096,256]{1,0:T(8,128)(2,1)} %param.17) | copy-start | bytes 6291460
  23.2 13.6 %collective-permute-start = (bf16[2,512,256]{2,1,0:T(8,128)(2,1)S(1)}, bf16[2,512,256]{2,1,0:T(8,128)(2,1)S(1)}, u32[]{:S(2)}, u32[]{:S(2)}) collective-permute-start(bf16[2,512,256]{2,1,0:T(8,128)(2,1)S(1)} %get-tuple-element.505), channel_id=1, source_target_pairs={{0,2},{2,4},{4,6},{6,8},{8,10},{10,12},{12,14},{14,16},{16,18},{18... | collective-permute-start | bytes 1572872 | tf_op jit(solution)/shard_map/while/body/eval_jaxpr/ppermute | solution.py:21
  37.6 13.6 %collective-permute-start = (bf16[2,512,256]{2,1,0:T(8,128)(2,1)S(1)}, bf16[2,512,256]{2,1,0:T(8,128)(2,1)S(1)}, u32[]{:S(2)}, u32[]{:S(2)}) collective-permute-start(bf16[2,512,256]{2,1,0:T(8,128)(2,1)S(1)} %get-tuple-element.505), channel_id=1, source_target_pairs={{0,2},{2,4},{4,6},{6,8},{8,10},{10,12},{12,14},{14,16},{16,18},{18... | collective-permute-start | bytes 1572872 | tf_op jit(solution)/shard_map/while/body/eval_jaxpr/ppermute | solution.py:21
  52.1 13.6 %collective-permute-start = (bf16[2,512,256]{2,1,0:T(8,128)(2,1)S(1)}, bf16[2,512,256]{2,1,0:T(8,128)(2,1)S(1)}, u32[]{:S(2)}, u32[]{:S(2)}) collective-permute-start(bf16[2,512,256]{2,1,0:T(8,128)(2,1)S(1)} %get-tuple-element.505), channel_id=1, source_target_pairs={{0,2},{2,4},{4,6},{6,8},{8,10},{10,12},{12,14},{14,16},{16,18},{18... | collective-permute-start | bytes 1572872 | tf_op jit(solution)/shard_map/while/body/eval_jaxpr/ppermute | solution.py:21
  66.6 13.6 %collective-permute-start = (bf16[2,512,256]{2,1,0:T(8,128)(2,1)S(1)}, bf16[2,512,256]{2,1,0:T(8,128)(2,1)S(1)}, u32[]{:S(2)}, u32[]{:S(2)}) collective-permute-start(bf16[2,512,256]{2,1,0:T(8,128)(2,1)S(1)} %get-tuple-element.505), channel_id=1, source_target_pairs={{0,2},{2,4},{4,6},{6,8},{8,10},{10,12},{12,14},{14,16},{16,18},{18... | collective-permute-start | bytes 1572872 | tf_op jit(solution)/shard_map/while/body/eval_jaxpr/ppermute | solution.py:21
  81.1 13.6 %collective-permute-start = (bf16[2,512,256]{2,1,0:T(8,128)(2,1)S(1)}, bf16[2,512,256]{2,1,0:T(8,128)(2,1)S(1)}, u32[]{:S(2)}, u32[]{:S(2)}) collective-permute-start(bf16[2,512,256]{2,1,0:T(8,128)(2,1)S(1)} %get-tuple-element.505), channel_id=1, source_target_pairs={{0,2},{2,4},{4,6},{6,8},{8,10},{10,12},{12,14},{14,16},{16,18},{18... | collective-permute-start | bytes 1572872 | tf_op jit(solution)/shard_map/while/body/eval_jaxpr/ppermute | solution.py:21
  95.6 13.6 %collective-permute-start = (bf16[2,512,256]{2,1,0:T(8,128)(2,1)S(1)}, bf16[2,512,256]{2,1,0:T(8,128)(2,1)S(1)}, u32[]{:S(2)}, u32[]{:S(2)}) collective-permute-start(bf16[2,512,256]{2,1,0:T(8,128)(2,1)S(1)} %get-tuple-element.505), channel_id=1, source_target_pairs={{0,2},{2,4},{4,6},{6,8},{8,10},{10,12},{12,14},{14,16},{16,18},{18... | collective-permute-start | bytes 1572872 | tf_op jit(solution)/shard_map/while/body/eval_jaxpr/ppermute | solution.py:21
  110.0 13.6 %collective-permute-start = (bf16[2,512,256]{2,1,0:T(8,128)(2,1)S(1)}, bf16[2,512,256]{2,1,0:T(8,128)(2,1)S(1)}, u32[]{:S(2)}, u32[]{:S(2)}) collective-permute-start(bf16[2,512,256]{2,1,0:T(8,128)(2,1)S(1)} %get-tuple-element.505), channel_id=1, source_target_pairs={{0,2},{2,4},{4,6},{6,8},{8,10},{10,12},{12,14},{14,16},{16,18},{18... | collective-permute-start | bytes 1572872 | tf_op jit(solution)/shard_map/while/body/eval_jaxpr/ppermute | solution.py:21
  124.5 13.6 %collective-permute-start = (bf16[2,512,256]{2,1,0:T(8,128)(2,1)S(1)}, bf16[2,512,256]{2,1,0:T(8,128)(2,1)S(1)}, u32[]{:S(2)}, u32[]{:S(2)}) collective-permute-start(bf16[2,512,256]{2,1,0:T(8,128)(2,1)S(1)} %get-tuple-element.505), channel_id=1, source_target_pairs={{0,2},{2,4},{4,6},{6,8},{8,10},{10,12},{12,14},{14,16},{16,18},{18... | collective-permute-start | bytes 1572872 | tf_op jit(solution)/shard_map/while/body/eval_jaxpr/ppermute | solution.py:21
  160.0 3.2 copy-start.8
  160.0 3.2 copy-start.9
  160.0 3.2 copy-start.10
  176.1 1.7 copy-start.6
  193.4 1.7 copy-start.6
  210.7 1.7 copy-start.6
  228.0 1.7 copy-start.6
  311.9 45.2 %all-to-all-start = ((bf16[2,512,2048]{2,1,0:T(8,128)(2,1)}), bf16[2,512,2048]{2,1,0:T(8,128)(2,1)}, u32[]{:S(2)}, u32[]{:S(2)}) async-start(bf16[2,512,2048]{2,1,0:T(8,128)(2,1)} %bitcast.99), calls=%async_computation | async-start | bytes 8388608 | tf_op jit(solution)/shard_map/all_to_all | solution.py:32
  357.1 4.6 %copy-start.3 = (f32[512,4096]{1,0:T(8,128)S(1)}, f32[512,4096]{1,0:T(8,128)}, u32[]{:S(2)}) copy-start(f32[512,4096]{1,0:T(8,128)} %convert_element_type.50) | copy-start | bytes 25165828
  357.1 6.6 %copy-start.1 = (bf16[4096,256]{1,0:T(8,128)(2,1)S(1)}, bf16[4096,256]{1,0:T(8,128)(2,1)}, u32[]{:S(2)}) copy-start(bf16[4096,256]{1,0:T(8,128)(2,1)} %param.16) | copy-start | bytes 6291460
  (4 other events, 6.7 us)
Sparse Core Ops, SparseCore 0:
  15.3 128.9 all-gather.3
where the time goes:
time: 373 us; the launch traced here: 371 us
  waiting for transfers between devices  126 us (34%)
  matrix products  82.2 us (22%)
  local copies, waits for them, and re-layouts  55.7 us (15%)
  other arithmetic  40.2 us (11%)
  loops' own time  31.5 us (8%)
  starting transfers between devices  20.9 us (6%)
  between operations  13.6 us (4%)
    ppermute x8, waiting for transfers between devices, shifted(): return lax.ppermute(shard, axis, pairs)  93.4 us
    dot_general x8, matrix products, one_head(): jnp.einsum('te,le->tl', head_queries, head_keys, preferred_element_type=j...  35.6 us
    all_to_all x1, waiting for transfers between devices, sent_and_summed(): lax.all_to_all(parts, axis, split_axis=0, concat_axis=0, tiled=True)  33.1 us
    another operation x1, loops' own time, attend(): per_head = lax.map(one_head, jnp.arange(heads_here, dtype=jnp.int32))  31.3 us
    ppermute x8, starting transfers between devices, shifted(): return lax.ppermute(shard, axis, pairs)  15.3 us
    dot_general x8, matrix products, one_head(): jnp.einsum('tl,le->te', weights, head_values, preferred_element_type=jnp....  12.7 us
    reduce_sum x8, other arithmetic, one_head(): jnp.sum(weights, axis=1, keepdims=True)  11.2 us
    dot_general x1, matrix products, local(): jnp.dot(normed, w_query, preferred_element_type=jnp.float32)  9.14 us
  transfers between devices with their start and end apart: 10, of which 9 were waited for; matrix products, arithmetic and copies ran while one was open for 11% of the time, Pallas kernels for 0%

commit v1 on v0

v1 whole, which is shorter than its diff:
```python
import functools

import jax
import jax.numpy as jnp
from jax import lax
from jax.experimental import pallas as pl
from jax.experimental.pallas import tpu as pltpu
from jax.sharding import PartitionSpec as P

MESH = pl.DeviceIdType.MESH
HD = 128
T = 512
D = 4096
SINK = 4
SROWS = 16
EPS = 1e-05
LOG2E = 1.4426950408889634
CSCALE = LOG2E * HD ** (-0.5)
NEG = -1e30
F32 = jnp.float32
BF16 = jnp.bfloat16
QT = 256

S_PREV, S_POS, S_NEG, S_FPOS, S_FNEG, S_D2D = 0, 1, 2, 3, 4, 5
N_HALO_SEND = S_D2D + 5


def kernel(
    x_hbm, gain_ref, wq_hbm, wk_hbm, wv_hbm, wo_hbm, win_ref, cnt_ref, bias_ref,
    out_hbm,
    x_v, n_v, wq_v, wkv_v, wown_v, wpeer_v, kv_v, sink_v, q_v, acc_v, m_v, rel_v,
    att_v, attp_v, o0_v, o1_v, out_v,
    in_sem, hsend, hrecv, wsend, wrecv, ssend, srecv, asend, arecv, out_sem,
):
    seq = lax.axis_index("seq")
    j = lax.axis_index("head")
    k = seq % 2
    x = (seq // 2) % 4
    r = seq // 8
    yl = r % 2
    z = r // 2
    peer = 1 - j

    def at(z_, yl_, x_, k_):
        return ((z_ * 2 + yl_) * 4 + x_) * 2 + k_

    sib = (at(z, yl, x, 1 - k), j)
    rn = (r + 1) % 8
    next_row = (rn * 8 + x * 2 + k, j)
    xp = (at(z, yl, (x + 1) % 4, k), j)
    xm = (at(z, yl, (x + 3) % 4, k), j)
    x2 = (at(z, yl, (x + 2) % 4, k), j)
    zp = (at((z + 1) % 4, yl, x, k), j)
    zm = (at((z + 3) % 4, yl, x, k), j)
    yo = (at(z, 1 - yl, x, k), j)
    head_peer = (seq, peer)

    def rcopy(src, dst, ss, rs, dev):
        return pltpu.make_async_remote_copy(
            src_ref=src, dst_ref=dst, send_sem=ss, recv_sem=rs, device_id=dev, device_id_type=MESH
        )

    def xcopy(i):
        rows = pl.ds(i * 128, 128)
        return pltpu.make_async_copy(x_hbm.at[rows], x_v.at[rows], in_sem.at[i])

    def kvcopy(i):
        g, w = i // 2, i % 2
        src = wk_hbm if w == 0 else wv_hbm
        return pltpu.make_async_copy(
            src.at[:, pl.ds(g * HD, HD)], wkv_v.at[:, pl.ds(i * HD, HD)], in_sem.at[4 + i]
        )

    def qcopy(i):
        cols = pl.ds(i * 256, 256)
        return pltpu.make_async_copy(wq_hbm.at[:, cols], wq_v.at[:, cols], in_sem.at[8 + i])

    own_copy = pltpu.make_async_copy(
        wo_hbm.at[:, pl.ds(pl.multiple_of(j * 2048, 2048), 2048)], wown_v, in_sem.at[12]
    )
    L = ((k * 4 + z) * 4 + x) * 2 + yl
    w0 = rcopy(
        wo_hbm.at[pl.ds(L * 16, 16), pl.ds(pl.multiple_of(peer * 2048, 2048), 2048)],
        wpeer_v.at[L], wsend.at[0], wrecv.at[0], head_peer,
    )
    w0.start()
    for i in range(4):
        xcopy(i).start()
    for i in range(4):
        kvcopy(i).start()
    for i in range(4):
        qcopy(i).start()
    own_copy.start()

    w1 = rcopy(wpeer_v.at[L], wpeer_v.at[L], wsend.at[1], wrecv.at[1], yo)
    L2 = ((k * 4 + z) * 4 + x) * 2
    two = wpeer_v.at[pl.ds(L2, 2)]
    w2 = [rcopy(two, two, wsend.at[2 + i], wrecv.at[2 + i], d) for i, d in enumerate((xp, xm, x2))]
    L8 = (k * 4 + z) * 8
    eight = wpeer_v.at[pl.ds(L8, 8)]
    w3 = [rcopy(eight, eight, wsend.at[5 + i], wrecv.at[5 + i], d) for i, d in enumerate((zp, zm))]
    Lm = (k * 4 + (z + 3) % 4) * 8
    Lp = (k * 4 + (z + 1) % 4) * 8
    lo4 = wpeer_v.at[pl.ds(Lm, 4)]
    hi4 = wpeer_v.at[pl.ds(Lp + 4, 4)]
    w4 = [rcopy(lo4, lo4, wsend.at[7], wrecv.at[7], zp), rcopy(hi4, hi4, wsend.at[8], wrecv.at[8], zm)]
    half = wpeer_v.at[pl.ds(k * 32, 32)]
    w5 = rcopy(half, half, wsend.at[9], wrecv.at[9], sib)

    own_slot = k
    prev_slot = 8 + k

    def slot_copy(src_slot, dst_slot, g, srow, dev, rslot):
        return rcopy(kv_v.at[src_slot, g], kv_v.at[dst_slot, g], hsend.at[g, srow], hrecv.at[g, rslot], dev)

    def c_prev(g):
        return slot_copy(own_slot, 8 + k, g, S_PREV, next_row, 8 + k)

    def c_pos(g, src):
        return slot_copy(src, 2 + k, g, S_POS, xp, 2 + k)

    def c_neg(g, src):
        return slot_copy(src, 6 + k, g, S_NEG, xm, 6 + k)

    def c_fpos(g):
        return slot_copy(2 + k, 4 + k, g, S_FPOS, xp, 4 + k)

    def c_fneg(g):
        return slot_copy(6 + k, 4 + k, g, S_FNEG, xm, 4 + k)

    def c_d2d(g, d):
        return slot_copy(2 * d + k, 2 * d + k, g, S_D2D + d, sib, 2 * d + k)

    def wait_slot(g, s):
        slot_copy(s, s, g, S_PREV, sib, s).wait_recv()

    mid = (x == 1) | (x == 2)

    def start_own(g):
        c_prev(g).start()

        @pl.when(x < 3)
        def _():
            c_pos(g, own_slot).start()

        @pl.when(x == 0)
        def _():
            c_neg(g, own_slot).start()

        @pl.when(k == 0)
        def _():
            c_d2d(g, 0).start()

    def f_prev(g):
        wait_slot(g, 8 + k)

        @pl.when(x == 3)
        def _():
            c_pos(g, prev_slot).start()

        @pl.when(x > 0)
        def _():
            c_neg(g, prev_slot).start()

        @pl.when(k == 1)
        def _():
            c_d2d(g, 4).start()

    def f_one(g):
        wait_slot(g, 2 + k)

        @pl.when(mid)
        def _():
            c_fpos(g).start()

        c_d2d(g, 1).start()

    def f_three(g):
        wait_slot(g, 6 + k)

        @pl.when(mid)
        def _():
            c_fneg(g).start()

        c_d2d(g, 3).start()

    def f_two(g):
        wait_slot(g, 4 + k)
        c_d2d(g, 2).start()

    def wait_sends(g):
        c_prev(g).wait_send()
        c_pos(g, own_slot).wait_send()
        c_neg(g, own_slot).wait_send()

        @pl.when(mid)
        def _():
            c_fpos(g).wait_send()
            c_fneg(g).wait_send()

        @pl.when(k == 0)
        def _():
            c_d2d(g, 0).wait_send()

        @pl.when(k == 1)
        def _():
            c_d2d(g, 4).wait_send()

        for d in (1, 2, 3):
            c_d2d(g, d).wait_send()

    sinks = sink_v.at[:]
    s_x = [rcopy(sinks, sinks, ssend.at[i], srecv.at[0], (at(0, 0, i + 1, 0), j)) for i in range(3)]
    s_y = rcopy(sinks, sinks, ssend.at[3], srecv.at[1], yo)
    s_z = [rcopy(sinks, sinks, ssend.at[4 + i], srecv.at[2], (at(i + 1, yl, x, 0), j)) for i in range(3)]
    s_k = rcopy(sinks, sinks, ssend.at[7], srecv.at[3], sib)
    is_root = seq == 0
    tier_x = (z == 0) & (yl == 0) & (k == 0)
    tier_y = (z == 0) & (k == 0)
    tier_z = k == 0

    def rel_rows(i, c):
        rows = pl.ds(i * 64, 64)
        a = lax.broadcasted_iota(jnp.int32, (64, T), 0) + i * 64
        b = lax.broadcasted_iota(jnp.int32, (64, T), 1)
        rel_v[rows, :] = a - b
        return c

    lax.fori_loop(0, 8, rel_rows, 0)
    gain = gain_ref[...]

    def norm_rows(i, c):
        rows = pl.ds(i * 32, 32)
        xt = x_v[rows, :].astype(F32)
        ms = jnp.mean(xt * xt, axis=1, keepdims=True)
        n_v[rows, :] = (xt * lax.rsqrt(ms + EPS) * gain).astype(BF16)
        return c

    for i in range(4):
        xcopy(i).wait()
        lax.fori_loop(i * 4, i * 4 + 4, norm_rows, 0)

    w0.wait_recv()
    w1.start()

    for g in range(2):
        kvcopy(2 * g).wait()
        kvcopy(2 * g + 1).wait()
        y = jnp.dot(n_v[...], wkv_v[:, g * 256 : g * 256 + 256], preferred_element_type=F32)
        kv_v[own_slot, g] = y.astype(BF16)
        start_own(g)

    @pl.when(is_root)
    def _():
        for g in range(2):
            sink_v[g] = kv_v[0, g, :SROWS, :]
        for c in s_x:
            c.start()

    w1.wait_recv()
    for c in w2:
        c.start()

    def q_tile(i):
        qcopy(i).wait()
        y = jnp.dot(n_v[...], wq_v[:, i * 256 : i * 256 + 256], preferred_element_type=F32)
        for h in range(2):
            qs = y[:, h * HD : h * HD + HD].astype(BF16).astype(F32) * CSCALE
            hi = qs.astype(BF16)
            q_v[2 * i + h, :, 0:HD] = hi
            q_v[2 * i + h, :, HD : 2 * HD] = (qs - hi.astype(F32)).astype(BF16)

    q_tile(0)
    q_tile(1)

    @pl.when(tier_x)
    def _():
        @pl.when(jnp.logical_not(is_root))
        def _():
            s_x[0].wait_recv()

        s_y.start()

    q_tile(2)
    q_tile(3)
    for c in w2:
        c.wait_recv()
    for c in w3:
        c.start()

    ones = jnp.ones((T, HD), BF16)
    nt = (((1,), (1,)), ((), ()))

    def tile_step(g, idx, slots, first):
        h = g * 4 + idx // 2
        rows = pl.ds(pl.multiple_of((idx % 2) * QT, QT), QT)
        q = q_v[h, rows, :]
        rel = rel_v[rows, :]
        w = win_ref[h]
        parts = []
        top = None
        for d, kk in slots:
            dist = 2 * d + k - kk
            keys = kv_v[2 * d + kk, g, :, 0:HD]
            s = lax.dot_general(
                q, jnp.concatenate([keys, keys], axis=1), nt, preferred_element_type=F32
            )
            limit = jnp.where(seq >= dist, w - T * dist, -100000)
            seen = rel < limit
            if first:
                seen = seen & (rel >= 0)
            s = jnp.where(seen, s, NEG)
            parts.append(s)
            t = jnp.max(s, axis=1, keepdims=True)
            top = t if top is None else jnp.maximum(top, t)
        if not first:
            old = m_v[h, rows, 0:1]
            top = jnp.maximum(top, old)
        total = None
        for (d, kk), s in zip(slots, parts):
            p = jnp.exp2(s - top).astype(BF16)
            vals = kv_v[2 * d + kk, g, :, HD : 2 * HD]
            o = jnp.dot(p, jnp.concatenate([vals, ones], axis=1), preferred_element_type=F32)
            total = o if total is None else total + o
        if not first:
            total = total + acc_v[h, rows, :] * jnp.exp2(old - top)
        acc_v[h, rows, :] = total
        m_v[h, rows, :] = jnp.broadcast_to(top, (QT, HD))

    def step(g, slots, first=False):
        def body(idx, c):
            tile_step(g, idx, slots, first)
            return c

        lax.fori_loop(0, 8, body, 0)

    def finish_tile(g, idx):
        h = g * 4 + idx // 2
        rows = pl.ds(pl.multiple_of((idx % 2) * QT, QT), QT)
        q = q_v[h, rows, :]
        ks = sink_v[g, :, 0:HD]
        vs = sink_v[g, :, HD : 2 * HD]
        s = lax.dot_general(q, jnp.concatenate([ks, ks], axis=1), nt, preferred_element_type=F32)
        s = s + bias_ref[h] * LOG2E
        col = lax.broadcasted_iota(jnp.int32, (QT, SROWS), 1)
        pos = lax.broadcasted_iota(jnp.int32, (QT, SROWS), 0) + (seq * T + (idx % 2) * QT)
        is_open = (col < cnt_ref[h]) & (col < SINK) & (col <= pos - win_ref[h])
        s = jnp.where(is_open, s, NEG)
        old = m_v[h, rows, 0:1]
        top = jnp.maximum(jnp.max(s, axis=1, keepdims=True), old)
        p = jnp.exp2(s - top).astype(BF16)
        o = jnp.dot(
            p, jnp.concatenate([vs, jnp.ones((SROWS, HD), BF16)], axis=1), preferred_element_type=F32
        )
        o = o + acc_v[h, rows, :] * jnp.exp2(old - top)
        return rows, (o[:, 0:HD] / o[:, HD : 2 * HD]).astype(BF16)

    def c_att(pair):
        return rcopy(att_v.at[pair], attp_v.at[pair], asend.at[pair], arecv.at[pair], head_peer)

    def finish(g):
        for pair in range(2):
            for h in range(2):
                for t in range(2):
                    rows, val = finish_tile(g, (pair * 2 + h) * 2 + t)
                    att_v[g * 2 + pair, rows, h * HD : h * HD + HD] = val
            c_att(g * 2 + pair).start()

    step(0, [(0, k)], first=True)
    f_prev(0)
    f_one(0)

    @pl.when(tier_y)
    def _():
        @pl.when(yl == 1)
        def _():
            s_y.wait_recv()

        @pl.when(z == 0)
        def _():
            for c in s_z:
                c.start()

    step(1, [(0, k)], first=True)
    special = jnp.where(k == 0, 4, 0)

    def wait_special(g):
        @pl.when(k == 1)
        def _():
            wait_slot(g, 0)

        @pl.when(k == 0)
        def _():
            wait_slot(g, 9)

    wait_special(0)
    step(0, [(special, 0), (4, 1)])
    f_three(0)
    f_prev(1)

    @pl.when(tier_z)
    def _():
        @pl.when(z > 0)
        def _():
            s_z[0].wait_recv()

        s_k.start()

    wait_slot(0, 2 + (1 - k))
    step(0, [(1, 0), (1, 1)])
    f_one(1)
    f_two(0)
    for c in w3:
        c.wait_recv()
    for c in w4:
        c.start()
    wait_slot(0, 6 + (1 - k))
    step(0, [(3, 0), (3, 1)])
    f_three(1)
    wait_slot(0, 4 + (1 - k))
    step(0, [(2, 0), (2, 1)])

    @pl.when(k == 1)
    def _():
        s_k.wait_recv()

    finish(0)
    wait_special(1)
    step(1, [(special, 0), (4, 1)])
    f_two(1)
    for c in w4:
        c.wait_recv()
    w5.start()
    wait_slot(1, 2 + (1 - k))
    step(1, [(1, 0), (1, 1)])
    wait_slot(1, 6 + (1 - k))
    step(1, [(3, 0), (3, 1)])
    wait_slot(1, 4 + (1 - k))
    step(1, [(2, 0), (2, 1)])
    finish(1)

    own_copy.wait()
    w5.wait_recv()
    NT_ = 512

    def proj_own(n, c):
        cols = pl.ds(pl.multiple_of(n * NT_, NT_), NT_)
        y = None
        for pr in range(4):
            o = jnp.dot(att_v[pr], wown_v[pr * 256 : pr * 256 + 256, cols], preferred_element_type=F32)
            y = o if y is None else y + o
        o0_v[:, cols] = y.astype(BF16)
        return c

    lax.fori_loop(0, 4, proj_own, 0)

    def wrows(pr, cols):
        return wpeer_v[pl.ds(pr * 16, 16), :, cols].reshape(256, NT_)

    for pr in range(2):
        c_att(pr).wait_recv()

    def proj_first(n, c):
        cols = pl.ds(pl.multiple_of(n * NT_, NT_), NT_)
        y = jnp.dot(attp_v[0], wrows(0, cols), preferred_element_type=F32)
        o1_v[:, cols] = y + jnp.dot(attp_v[1], wrows(1, cols), preferred_element_type=F32)
        return c

    lax.fori_loop(0, 4, proj_first, 0)
    for pr in range(2, 4):
        c_att(pr).wait_recv()

    def ocopy(n):
        cols = pl.ds(pl.multiple_of(n * NT_, NT_), NT_)
        return pltpu.make_async_copy(out_v.at[:, cols], out_hbm.at[:, cols], out_sem.at[n])

    def proj_last(n, c):
        cols = pl.ds(pl.multiple_of(n * NT_, NT_), NT_)
        y = jnp.dot(attp_v[2], wrows(2, cols), preferred_element_type=F32)
        y = y + jnp.dot(attp_v[3], wrows(3, cols), preferred_element_type=F32)
        y = (y + o1_v[:, cols]).astype(BF16).astype(F32)
        base = x_v[:, pl.ds(pl.multiple_of(j * 2048 + n * NT_, NT_), NT_)].astype(F32)
        out_v[:, cols] = (base + (o0_v[:, cols].astype(F32) + y)).astype(BF16)
        ocopy(n).start()
        return c

    lax.fori_loop(0, 4, proj_last, 0)

    for g in range(2):
        wait_sends(g)
    w0.wait_send()
    w1.wait_send()
    for c in w2 + w3 + w4:
        c.wait_send()
    w5.wait_send()

    @pl.when(is_root)
    def _():
        for c in s_x:
            c.wait_send()

    @pl.when(tier_x)
    def _():
        s_y.wait_send()

    @pl.when(tier_y)
    def _():
        for c in s_z:
            c.wait_send()

    @pl.when(tier_z)
    def _():
        s_k.wait_send()

    for pr in range(4):
        c_att(pr).wait_send()
    for n in range(4):
        ocopy(n).wait()


def local(tokens, norm_gain, w_query, w_key, w_value, w_out, window, sink_count, sink_bias):
    any_ = pl.BlockSpec(memory_space=pl.ANY)
    smem = pl.BlockSpec(memory_space=pltpu.SMEM)
    vmem = pl.BlockSpec(memory_space=pltpu.VMEM)
    dma = pltpu.SemaphoreType.DMA
    return pl.pallas_call(
        kernel,
        out_shape=jax.ShapeDtypeStruct((T, 2048), BF16),
        in_specs=[any_, vmem, any_, any_, any_, any_, smem, smem, smem],
        out_specs=any_,
        scratch_shapes=[
            pltpu.VMEM((T, D), BF16),
            pltpu.VMEM((T, D), BF16),
            pltpu.VMEM((D, 1024), BF16),
            pltpu.VMEM((D, 512), BF16),
            pltpu.VMEM((1024, 2048), BF16),
            pltpu.VMEM((64, 16, 2048), BF16),
            pltpu.VMEM((10, 2, T, 256), BF16),
            pltpu.VMEM((2, SROWS, 256), BF16),
            pltpu.VMEM((8, T, 256), BF16),
            pltpu.VMEM((8, T, 256), F32),
            pltpu.VMEM((8, T, HD), F32),
            pltpu.VMEM((T, T), jnp.int32),
            pltpu.VMEM((4, T, 256), BF16),
            pltpu.VMEM((4, T, 256), BF16),
            pltpu.VMEM((T, 2048), BF16),
            pltpu.VMEM((T, 2048), F32),
            pltpu.VMEM((T, 2048), BF16),
            dma((13,)),
            dma((2, N_HALO_SEND)),
            dma((2, 10)),
            dma((10,)),
            dma((10,)),
            dma((8,)),
            dma((4,)),
            dma((4,)),
            dma((4,)),
            dma((4,)),
        ],
        compiler_params=pltpu.CompilerParams(
            has_side_effects=True, vmem_limit_bytes=64 * 1024 * 1024 - 65536
        ),
        name="block",
    )(tokens, norm_gain.reshape(1, D), w_query, w_key, w_value, w_out, window, sink_count, sink_bias)


def solution(mesh):
    in_specs = (
        P("seq", None),
        P(),
        P(None, "head"),
        P(None, "head"),
        P(None, "head"),
        P("head", None),
        P("head"),
        P("head"),
        P("head"),
    )
    return jax.shard_map(local, mesh=mesh, in_specs=in_specs, out_specs=P("seq", "head"), check_vma=False)
```

time: 373 us -> 145 us (0.39)
  Pallas kernels: 0 us -> 142 us
  waiting for transfers between devices: 126 us -> 0 us
  matrix products: 82.2 us -> 0 us
  local copies, waits for them, and re-layouts: 55.7 us -> 3.16 us
  other arithmetic: 40.2 us -> 0 us
  loops' own time: 31.5 us -> 0 us
  starting transfers between devices: 20.9 us -> 0 us
  between operations: 13.6 us -> 0.01 us
    pallas_call x0 -> x1, Pallas kernels: none -> 142 us  [local(): pl.pallas_call(kernel, out_shape=jax.ShapeDtypeStruct((T, 2048), BF16), i...]
    ppermute x8 -> x0, waiting for transfers between devices: 93.4 us -> none  [shifted(): return lax.ppermute(shard, axis, pairs)]
    dot_general x38 -> x0, matrix products: 82.2 us -> none  [the longest x8 35.6 us: one_head(): jnp.einsum('te,le->tl', head_queries, head_keys, preferred_element_type=j...]
    all_to_all x1 -> x0, waiting for transfers between devices: 33.1 us -> none  [sent_and_summed(): lax.all_to_all(parts, axis, split_axis=0, concat_axis=0, tiled=True)]
    another operation x2 -> x0, loops' own time: 31.5 us -> none  [the longest x1 31.3 us: attend(): per_head = lax.map(one_head, jnp.arange(heads_here, dtype=jnp.int32))]
    dynamic_slice x32 -> x0, local copies, waits for them, and re-layouts: 19.6 us -> none  [the longest x8 4.92 us: one_head(): open_sinks = sink_count[index]]
    reduce_sum x18 -> x0, other arithmetic: 18.5 us -> none  [the longest x8 11.2 us: one_head(): jnp.sum(weights, axis=1, keepdims=True)]
    dynamic_update_slice x25 -> x0, local copies, waits for them, and re-layouts: 15.5 us -> none  [the longest x8 6.79 us: advance(): lax.dynamic_update_slice_in_dim(gathered, moving, (SPAN - 2 - offset) * t...]
  transfers between devices with their start and end apart: 10 -> 0, of which waited for: 9 -> 0; matrix products, arithmetic and copies ran while one was open for 11% -> 0% of each run, Pallas kernels for 0% -> 0%
where the time goes in v1:
time: 145 us
  Pallas kernels  142 us (98%)
  local copies, waits for them, and re-layouts  3.16 us (2%)
    pallas_call x1, Pallas kernels, local(): pl.pallas_call(kernel, out_shape=jax.ShapeDtypeStruct((T, 2048), BF16), i...  142 us
    unnamed x1, local copies, waits for them, and re-layouts  3.16 us

profile of v1, /device:TPU:96, one launch (start us, length us, event | category | flops | bytes accessed | tf_op | source)
XLA Modules:
  0.0 144.9 jit_solution(11367181988579928541)
XLA Ops:
  0.0 141.8 %block.1 = bf16[512,2048]{1,0:T(8,128)(2,1)} custom-call(bf16[512,4096]{1,0:T(8,128)(2,1)} %x_hbm.1, f32[1,4096]{1,0:T(1,128)} %bitcast.1, bf16[4096,1024]{1,0:T(8,128)(2,1)} %wq_hbm.1, bf16[4096,256]{1,0:T(8,128)(2,1)} %wk_hbm.1, bf16[4096,256]{1,0:T(8,128)(2,1)} %wv_hbm.1, bf16[1024,4096]{1,0:T(8,128)(2,1)} %wo_hbm.1, s32[8]{0:T(128)} %win_ref.1, ...), custom_call_target="tpu_custom_call" | custom-call | tf_op jit(solution)/shard_map/block/pallas_call | solution.py:526
  141.8 3.2 %copy.11 = bf16[512,2048]{1,0:T(8,128)(2,1)} copy(bf16[512,2048]{1,0:T(8,128)(2,1)} %block.1) | data formatting | bytes 4194304

commit v2 on v1

--- a/solution.py
+++ b/solution.py
@@ -14,12 +14,13 @@
 SINK = 4
 SROWS = 16
 EPS = 1e-05
+scope = jax.named_scope
 LOG2E = 1.4426950408889634
 CSCALE = LOG2E * HD ** (-0.5)
 NEG = -1e30
 F32 = jnp.float32
 BF16 = jnp.bfloat16
-QT = 256
+VR = 144
 
 S_PREV, S_POS, S_NEG, S_FPOS, S_FNEG, S_D2D = 0, 1, 2, 3, 4, 5
 N_HALO_SEND = S_D2D + 5
@@ -28,7 +29,7 @@
 def kernel(
     x_hbm, gain_ref, wq_hbm, wk_hbm, wv_hbm, wo_hbm, win_ref, cnt_ref, bias_ref,
     out_hbm,
-    x_v, n_v, wq_v, wkv_v, wown_v, wpeer_v, kv_v, sink_v, q_v, acc_v, m_v, rel_v,
+    x_v, n_v, wq_v, wkv_v, wown_v, wpeer_v, kv_v, sink_v, q_v, acc_v, m_v, rel_v, sa_v, sb_v,
     att_v, attp_v, o0_v, o1_v, out_v,
     in_sem, hsend, hrecv, wsend, wrecv, ssend, srecv, asend, arecv, out_sem,
 ):
@@ -78,12 +79,6 @@
     own_copy = pltpu.make_async_copy(
         wo_hbm.at[:, pl.ds(pl.multiple_of(j * 2048, 2048), 2048)], wown_v, in_sem.at[12]
     )
-    L = ((k * 4 + z) * 4 + x) * 2 + yl
-    w0 = rcopy(
-        wo_hbm.at[pl.ds(L * 16, 16), pl.ds(pl.multiple_of(peer * 2048, 2048), 2048)],
-        wpeer_v.at[L], wsend.at[0], wrecv.at[0], head_peer,
-    )
-    w0.start()
     for i in range(4):
         xcopy(i).start()
     for i in range(4):
@@ -91,6 +86,18 @@
     for i in range(4):
         qcopy(i).start()
     own_copy.start()
+
+    z2 = (at((z + 2) % 4, yl, x, k), j)
+    prev_row = (((r + 7) % 8) * 8 + x * 2 + k, j)
+    barrier = pltpu.get_barrier_semaphore()
+    for dev in (sib, prev_row, xp, xm, x2, zp, zm, z2, yo, head_peer):
+        pl.semaphore_signal(barrier, inc=1, device_id=dev, device_id_type=MESH)
+
+    L = ((k * 4 + z) * 4 + x) * 2 + yl
+    w0 = rcopy(
+        wo_hbm.at[pl.ds(L * 16, 16), pl.ds(pl.multiple_of(peer * 2048, 2048), 2048)],
+        wpeer_v.at[L], wsend.at[0], wrecv.at[0], head_peer,
+    )
 
     w1 = rcopy(wpeer_v.at[L], wpeer_v.at[L], wsend.at[1], wrecv.at[1], yo)
     L2 = ((k * 4 + z) * 4 + x) * 2
@@ -166,14 +173,16 @@
         def _():
             c_d2d(g, 4).start()
 
-    def f_one(g):
-        wait_slot(g, 2 + k)
-
-        @pl.when(mid)
-        def _():
-            c_fpos(g).start()
-
-        c_d2d(g, 1).start()
+    def f_one(g, early):
+        @pl.when((x > 0) if early else (x == 0))
+        def _():
+            wait_slot(g, 2 + k)
+
+            @pl.when(mid)
+            def _():
+                c_fpos(g).start()
+
+            c_d2d(g, 1).start()
 
     def f_three(g):
         wait_slot(g, 6 + k)
@@ -223,11 +232,15 @@
         rows = pl.ds(i * 64, 64)
         a = lax.broadcasted_iota(jnp.int32, (64, T), 0) + i * 64
         b = lax.broadcasted_iota(jnp.int32, (64, T), 1)
-        rel_v[rows, :] = a - b
+        rel_v[rows, :] = b - a
         return c
 
-    lax.fori_loop(0, 8, rel_rows, 0)
+    with scope("rel_rows"):
+        lax.fori_loop(0, 8, rel_rows, 0)
     gain = gain_ref[...]
+    with scope("barrier"):
+        pl.semaphore_wait(barrier, 10)
+    w0.start()
 
     def norm_rows(i, c):
         rows = pl.ds(i * 32, 32)
@@ -237,41 +250,48 @@
         return c
 
     for i in range(4):
-        xcopy(i).wait()
-        lax.fori_loop(i * 4, i * 4 + 4, norm_rows, 0)
-
-    w0.wait_recv()
-    w1.start()
+        with scope("xwait"):
+            xcopy(i).wait()
+        with scope("norm"):
+            lax.fori_loop(i * 4, i * 4 + 4, norm_rows, 0)
 
     for g in range(2):
-        kvcopy(2 * g).wait()
-        kvcopy(2 * g + 1).wait()
+        with scope("kvwait"):
+            kvcopy(2 * g).wait()
+            kvcopy(2 * g + 1).wait()
         y = jnp.dot(n_v[...], wkv_v[:, g * 256 : g * 256 + 256], preferred_element_type=F32)
-        kv_v[own_slot, g] = y.astype(BF16)
+        kv_v[own_slot, g, :, 0:HD] = y[:, 0:HD].astype(BF16)
+        for c in range(4):
+            kv_v[own_slot, g, c * HD : c * HD + HD, HD : 2 * HD] = (
+                y[c * HD : c * HD + HD, HD : 2 * HD].T.astype(BF16)
+            )
         start_own(g)
 
+        @pl.when(is_root)
+        def _():
+            sink_v[g] = y[:SROWS, :].astype(BF16)
+
     @pl.when(is_root)
     def _():
-        for g in range(2):
-            sink_v[g] = kv_v[0, g, :SROWS, :]
         for c in s_x:
             c.start()
 
-    w1.wait_recv()
-    for c in w2:
-        c.start()
+    with scope("w0_wait_recv"):
+        w0.wait_recv()
+    w1.start()
 
     def q_tile(i):
-        qcopy(i).wait()
-        y = jnp.dot(n_v[...], wq_v[:, i * 256 : i * 256 + 256], preferred_element_type=F32)
-        for h in range(2):
-            qs = y[:, h * HD : h * HD + HD].astype(BF16).astype(F32) * CSCALE
-            hi = qs.astype(BF16)
-            q_v[2 * i + h, :, 0:HD] = hi
-            q_v[2 * i + h, :, HD : 2 * HD] = (qs - hi.astype(F32)).astype(BF16)
-
-    q_tile(0)
-    q_tile(1)
+        qcopy(2 * i).wait()
+        qcopy(2 * i + 1).wait()
+        y = jnp.dot(n_v[...], wq_v[:, i * 512 : i * 512 + 512], preferred_element_type=F32)
+        for h in range(4):
+            qt = y[:, h * HD : h * HD + HD].astype(BF16).astype(F32).T * CSCALE
+            hi = qt.astype(BF16)
+            q_v[4 * i + h, 0:HD, :] = hi
+            q_v[4 * i + h, HD : 2 * HD, :] = (qt - hi.astype(F32)).astype(BF16)
+
+    with scope("q0"):
+        q_tile(0)
 
     @pl.when(tier_x)
     def _():
@@ -281,107 +301,84 @@
 
         s_y.start()
 
-    q_tile(2)
-    q_tile(3)
-    for c in w2:
-        c.wait_recv()
-    for c in w3:
-        c.start()
-
-    ones = jnp.ones((T, HD), BF16)
-    nt = (((1,), (1,)), ((), ()))
-
-    def tile_step(g, idx, slots, first):
-        h = g * 4 + idx // 2
-        rows = pl.ds(pl.multiple_of((idx % 2) * QT, QT), QT)
-        q = q_v[h, rows, :]
-        rel = rel_v[rows, :]
+    ones = jnp.ones((VR - HD, T), BF16)
+
+    def values_t(slot, g):
+        vt = [kv_v[slot, g, c * HD : c * HD + HD, HD : 2 * HD] for c in range(4)]
+        return jnp.concatenate([jnp.concatenate(vt, axis=1), ones], axis=0)
+
+    def scores(g, h, slots, first, s_ref):
+        q = q_v[h]
         w = win_ref[h]
-        parts = []
         top = None
-        for d, kk in slots:
+        for b, (d, kk) in enumerate(slots):
             dist = 2 * d + k - kk
             keys = kv_v[2 * d + kk, g, :, 0:HD]
-            s = lax.dot_general(
-                q, jnp.concatenate([keys, keys], axis=1), nt, preferred_element_type=F32
-            )
+            s = jnp.dot(jnp.concatenate([keys, keys], axis=1), q, preferred_element_type=F32)
             limit = jnp.where(seq >= dist, w - T * dist, -100000)
+            rel = rel_v[...]
             seen = rel < limit
             if first:
                 seen = seen & (rel >= 0)
             s = jnp.where(seen, s, NEG)
-            parts.append(s)
-            t = jnp.max(s, axis=1, keepdims=True)
+            s_ref[b * T : b * T + T, :] = s
+            t = jnp.max(s, axis=0, keepdims=True)
             top = t if top is None else jnp.maximum(top, t)
+        return top
+
+    def weigh(g, h, slots, first, s_ref, top):
         if not first:
-            old = m_v[h, rows, 0:1]
+            old = m_v[h, 0:1, :]
             top = jnp.maximum(top, old)
         total = None
-        for (d, kk), s in zip(slots, parts):
-            p = jnp.exp2(s - top).astype(BF16)
-            vals = kv_v[2 * d + kk, g, :, HD : 2 * HD]
-            o = jnp.dot(p, jnp.concatenate([vals, ones], axis=1), preferred_element_type=F32)
+        for b, (d, kk) in enumerate(slots):
+            p = jnp.exp2(s_ref[b * T : b * T + T, :] - top).astype(BF16)
+            o = jnp.dot(values_t(2 * d + kk, g), p, preferred_element_type=F32)
             total = o if total is None else total + o
         if not first:
-            total = total + acc_v[h, rows, :] * jnp.exp2(old - top)
-        acc_v[h, rows, :] = total
-        m_v[h, rows, :] = jnp.broadcast_to(top, (QT, HD))
+            total = total + acc_v[h] * jnp.exp2(old - top)
+        acc_v[h] = total
+        m_v[h] = jnp.broadcast_to(top, (8, T))
 
     def step(g, slots, first=False):
-        def body(idx, c):
-            tile_step(g, idx, slots, first)
-            return c
-
-        lax.fori_loop(0, 8, body, 0)
-
-    def finish_tile(g, idx):
-        h = g * 4 + idx // 2
-        rows = pl.ds(pl.multiple_of((idx % 2) * QT, QT), QT)
-        q = q_v[h, rows, :]
-        ks = sink_v[g, :, 0:HD]
-        vs = sink_v[g, :, HD : 2 * HD]
-        s = lax.dot_general(q, jnp.concatenate([ks, ks], axis=1), nt, preferred_element_type=F32)
-        s = s + bias_ref[h] * LOG2E
-        col = lax.broadcasted_iota(jnp.int32, (QT, SROWS), 1)
-        pos = lax.broadcasted_iota(jnp.int32, (QT, SROWS), 0) + (seq * T + (idx % 2) * QT)
-        is_open = (col < cnt_ref[h]) & (col < SINK) & (col <= pos - win_ref[h])
-        s = jnp.where(is_open, s, NEG)
-        old = m_v[h, rows, 0:1]
-        top = jnp.maximum(jnp.max(s, axis=1, keepdims=True), old)
-        p = jnp.exp2(s - top).astype(BF16)
-        o = jnp.dot(
-            p, jnp.concatenate([vs, jnp.ones((SROWS, HD), BF16)], axis=1), preferred_element_type=F32
-        )
-        o = o + acc_v[h, rows, :] * jnp.exp2(old - top)
-        return rows, (o[:, 0:HD] / o[:, HD : 2 * HD]).astype(BF16)
+        base = g * 4
+
+        def body(i, top):
+            h = base + 2 * i
+            top_b = scores(g, h + 1, slots, first, sb_v)
+            weigh(g, h, slots, first, sa_v, top)
+            top = scores(g, jnp.minimum(h + 2, base + 3), slots, first, sa_v)
+            weigh(g, h + 1, slots, first, sb_v, top_b)
+            return top
+
+        lax.fori_loop(0, 2, body, scores(g, base, slots, first, sa_v))
 
     def c_att(pair):
         return rcopy(att_v.at[pair], attp_v.at[pair], asend.at[pair], arecv.at[pair], head_peer)
+
+    def finish_head(g, h):
+        ks = sink_v[g, :, 0:HD]
+        vt = sink_v[g, :, HD : 2 * HD].astype(F32).T.astype(BF16)
+        s = jnp.dot(jnp.concatenate([ks, ks], axis=1), q_v[h], preferred_element_type=F32)
+        s = s + bias_ref[h] * LOG2E
+        row = lax.broadcasted_iota(jnp.int32, (SROWS, T), 0)
+        pos = lax.broadcasted_iota(jnp.int32, (SROWS, T), 1) + seq * T
+        is_open = (row < cnt_ref[h]) & (row < SINK) & (row <= pos - win_ref[h])
+        s = jnp.where(is_open, s, NEG)
+        old = m_v[h, 0:1, :]
+        top = jnp.maximum(jnp.max(s, axis=0, keepdims=True), old)
+        p = jnp.exp2(s - top)
+        scale = jnp.exp2(old - top)
+        total = acc_v[h, HD : HD + 1, :] * scale + jnp.sum(p, axis=0, keepdims=True)
+        o = acc_v[h, 0:HD, :] * scale + jnp.dot(vt, p.astype(BF16), preferred_element_type=F32)
+        return (o / total).T.astype(BF16)
 
     def finish(g):
         for pair in range(2):
             for h in range(2):
-                for t in range(2):
-                    rows, val = finish_tile(g, (pair * 2 + h) * 2 + t)
-                    att_v[g * 2 + pair, rows, h * HD : h * HD + HD] = val
+                att_v[g * 2 + pair, :, h * HD : h * HD + HD] = finish_head(g, g * 4 + pair * 2 + h)
             c_att(g * 2 + pair).start()
 
-    step(0, [(0, k)], first=True)
-    f_prev(0)
-    f_one(0)
-
-    @pl.when(tier_y)
-    def _():
-        @pl.when(yl == 1)
-        def _():
-            s_y.wait_recv()
-
-        @pl.when(z == 0)
-        def _():
-            for c in s_z:
-                c.start()
-
-    step(1, [(0, k)], first=True)
     special = jnp.where(k == 0, 4, 0)
 
     def wait_special(g):
@@ -393,10 +390,51 @@
         def _():
             wait_slot(g, 9)
 
-    wait_special(0)
-    step(0, [(special, 0), (4, 1)])
-    f_three(0)
-    f_prev(1)
+    with scope("q1"):
+        q_tile(1)
+    with scope("own0"):
+        step(0, [(0, k)], first=True)
+    with scope("f_prev0"):
+        f_prev(0)
+    with scope("f_one0"):
+        f_one(0, True)
+    with scope("w1_wait_recv"):
+        w1.wait_recv()
+    for c in w2:
+        c.start()
+    with scope("own1"):
+        step(1, [(0, k)], first=True)
+
+    @pl.when(tier_y)
+    def _():
+        @pl.when(yl == 1)
+        def _():
+            s_y.wait_recv()
+
+        for c in s_z:
+            c.start()
+
+    with scope("f_prev1"):
+        f_prev(1)
+    with scope("f_one1"):
+        f_one(1, True)
+    with scope("wsp0"):
+        wait_special(0)
+    with scope("step0sp"):
+        step(0, [(special, 0), (4, 1)])
+    with scope("w2wait"):
+        for c in w2:
+            c.wait_recv()
+    for c in w3:
+        c.start()
+    with scope("f_one0b"):
+        f_one(0, False)
+    with scope("f_three0"):
+        f_three(0)
+    with scope("w0_1"):
+        wait_slot(0, 2 + (1 - k))
+    with scope("step0_1"):
+        step(0, [(1, 0), (1, 1)])
 
     @pl.when(tier_z)
     def _():
@@ -406,41 +444,58 @@
 
         s_k.start()
 
-    wait_slot(0, 2 + (1 - k))
-    step(0, [(1, 0), (1, 1)])
-    f_one(1)
-    f_two(0)
-    for c in w3:
-        c.wait_recv()
+    with scope("f_one1b"):
+        f_one(1, False)
+    with scope("f_three1"):
+        f_three(1)
+    with scope("w0_3"):
+        wait_slot(0, 6 + (1 - k))
+    with scope("step0_3"):
+        step(0, [(3, 0), (3, 1)])
+    with scope("f_two0"):
+        f_two(0)
+    with scope("w3wait"):
+        for c in w3:
+            c.wait_recv()
     for c in w4:
         c.start()
-    wait_slot(0, 6 + (1 - k))
-    step(0, [(3, 0), (3, 1)])
-    f_three(1)
-    wait_slot(0, 4 + (1 - k))
-    step(0, [(2, 0), (2, 1)])
+    with scope("w0_2"):
+        wait_slot(0, 4 + (1 - k))
+    with scope("step0_2"):
+        step(0, [(2, 0), (2, 1)])
 
     @pl.when(k == 1)
     def _():
         s_k.wait_recv()
 
-    finish(0)
-    wait_special(1)
-    step(1, [(special, 0), (4, 1)])
-    f_two(1)
-    for c in w4:
-        c.wait_recv()
+    with scope("finish0"):
+        finish(0)
+    with scope("w1_1"):
+        wait_special(1)
+        wait_slot(1, 2 + (1 - k))
+    with scope("step1a"):
+        step(1, [(special, 0), (4, 1), (1, 0)])
+    with scope("f_two1"):
+        f_two(1)
+    with scope("w4wait"):
+        for c in w4:
+            c.wait_recv()
     w5.start()
-    wait_slot(1, 2 + (1 - k))
-    step(1, [(1, 0), (1, 1)])
-    wait_slot(1, 6 + (1 - k))
-    step(1, [(3, 0), (3, 1)])
-    wait_slot(1, 4 + (1 - k))
-    step(1, [(2, 0), (2, 1)])
-    finish(1)
-
-    own_copy.wait()
-    w5.wait_recv()
+    with scope("w1_3"):
+        wait_slot(1, 6 + (1 - k))
+    with scope("step1b"):
+        step(1, [(1, 1), (3, 0), (3, 1)])
+    with scope("w1_2"):
+        wait_slot(1, 4 + (1 - k))
+    with scope("step1c"):
+        step(1, [(2, 0), (2, 1)])
+    with scope("finish1"):
+        finish(1)
+
+    with scope("own_copy_wait"):
+        own_copy.wait()
+    with scope("w5_wait_recv"):
+        w5.wait_recv()
     NT_ = 512
 
     def proj_own(n, c):
@@ -452,13 +507,15 @@
         o0_v[:, cols] = y.astype(BF16)
         return c
 
-    lax.fori_loop(0, 4, proj_own, 0)
+    with scope("proj_own"):
+        lax.fori_loop(0, 4, proj_own, 0)
 
     def wrows(pr, cols):
         return wpeer_v[pl.ds(pr * 16, 16), :, cols].reshape(256, NT_)
 
-    for pr in range(2):
-        c_att(pr).wait_recv()
+    with scope("att01wait"):
+        for pr in range(2):
+            c_att(pr).wait_recv()
 
     def proj_first(n, c):
         cols = pl.ds(pl.multiple_of(n * NT_, NT_), NT_)
@@ -466,9 +523,11 @@
         o1_v[:, cols] = y + jnp.dot(attp_v[1], wrows(1, cols), preferred_element_type=F32)
         return c
 
-    lax.fori_loop(0, 4, proj_first, 0)
-    for pr in range(2, 4):
-        c_att(pr).wait_recv()
+    with scope("proj_first"):
+        lax.fori_loop(0, 4, proj_first, 0)
+    with scope("att23wait"):
+        for pr in range(2, 4):
+            c_att(pr).wait_recv()
 
     def ocopy(n):
         cols = pl.ds(pl.multiple_of(n * NT_, NT_), NT_)
@@ -484,7 +543,8 @@
         ocopy(n).start()
         return c
 
-    lax.fori_loop(0, 4, proj_last, 0)
+    with scope("proj_last"):
+        lax.fori_loop(0, 4, proj_last, 0)
 
     for g in range(2):
         wait_sends(g)
@@ -537,10 +597,12 @@
             pltpu.VMEM((64, 16, 2048), BF16),
             pltpu.VMEM((10, 2, T, 256), BF16),
             pltpu.VMEM((2, SROWS, 256), BF16),
-            pltpu.VMEM((8, T, 256), BF16),
-            pltpu.VMEM((8, T, 256), F32),
-            pltpu.VMEM((8, T, HD), F32),
+            pltpu.VMEM((8, 256, T), BF16),
+            pltpu.VMEM((8, VR, T), F32),
+            pltpu.VMEM((8, 8, T), F32),
             pltpu.VMEM((T, T), jnp.int32),
+            pltpu.VMEM((3 * T, T), F32),
+            pltpu.VMEM((3 * T, T), F32),
             pltpu.VMEM((4, T, 256), BF16),
             pltpu.VMEM((4, T, 256), BF16),
             pltpu.VMEM((T, 2048), BF16),
@@ -558,7 +620,7 @@
             dma((4,)),
         ],
         compiler_params=pltpu.CompilerParams(
-            has_side_effects=True, vmem_limit_bytes=64 * 1024 * 1024 - 65536
+            has_side_effects=True, collective_id=0, vmem_limit_bytes=64 * 1024 * 1024 - 65536
         ),
         name="block",
     )(tokens, norm_gain.reshape(1, D), w_query, w_key, w_value, w_out, window, sink_count, sink_bias)

time: 145 us -> 91.1 us (0.63)
  the two profiles are of different devices: /device:TPU:96 before, /device:TPU:1 now
where the time goes in v2:
time: 91.1 us; the launch traced here: 90.9 us
  Pallas kernels  87.7 us (96%)
  local copies, waits for them, and re-layouts  3.16 us (3%)
    pallas_call x1, Pallas kernels, local(): pl.pallas_call(kernel, out_shape=jax.ShapeDtypeStruct((T, 2048), BF16), i...  87.7 us
    unnamed x1, local copies, waits for them, and re-layouts  3.16 us

profile of v2, /device:TPU:1, one launch (start us, length us, event | category | flops | bytes accessed | tf_op | source)
XLA Modules:
  0.0 90.9 jit_solution(4545759619542954676)
XLA Ops:
  0.0 87.7 %block.1 = bf16[512,2048]{1,0:T(8,128)(2,1)} custom-call(bf16[512,4096]{1,0:T(8,128)(2,1)} %x_hbm.1, f32[1,4096]{1,0:T(1,128)} %bitcast.1, bf16[4096,1024]{1,0:T(8,128)(2,1)} %wq_hbm.1, bf16[4096,256]{1,0:T(8,128)(2,1)} %wk_hbm.1, bf16[4096,256]{1,0:T(8,128)(2,1)} %wv_hbm.1, bf16[1024,4096]{1,0:T(8,128)(2,1)} %wo_hbm.1, s32[8]{0:T(128)} %win_ref.1, ...), custom_call_target="tpu_custom_call" | custom-call | tf_op jit(solution)/shard_map/block/pallas_call | solution.py:586
  87.7 3.2 %copy.11 = bf16[512,2048]{1,0:T(8,128)(2,1)} copy(bf16[512,2048]{1,0:T(8,128)(2,1)} %block.1) | data formatting | bytes 4194304

commit v3 on v2

--- a/solution.py
+++ b/solution.py
@@ -55,6 +55,7 @@
     zm = (at((z + 3) % 4, yl, x, k), j)
     yo = (at(z, 1 - yl, x, k), j)
     head_peer = (seq, peer)
+    diag = (at(z, 1 - yl, x, k), peer)
 
     def rcopy(src, dst, ss, rs, dev):
         return pltpu.make_async_remote_copy(
@@ -90,29 +91,35 @@
     z2 = (at((z + 2) % 4, yl, x, k), j)
     prev_row = (((r + 7) % 8) * 8 + x * 2 + k, j)
     barrier = pltpu.get_barrier_semaphore()
-    for dev in (sib, prev_row, xp, xm, x2, zp, zm, z2, yo, head_peer):
+    for dev in (sib, prev_row, xp, xm, x2, zp, zm, z2, yo, head_peer, diag):
         pl.semaphore_signal(barrier, inc=1, device_id=dev, device_id_type=MESH)
 
-    L = ((k * 4 + z) * 4 + x) * 2 + yl
-    w0 = rcopy(
-        wo_hbm.at[pl.ds(L * 16, 16), pl.ds(pl.multiple_of(peer * 2048, 2048), 2048)],
-        wpeer_v.at[L], wsend.at[0], wrecv.at[0], head_peer,
-    )
-
-    w1 = rcopy(wpeer_v.at[L], wpeer_v.at[L], wsend.at[1], wrecv.at[1], yo)
-    L2 = ((k * 4 + z) * 4 + x) * 2
-    two = wpeer_v.at[pl.ds(L2, 2)]
-    w2 = [rcopy(two, two, wsend.at[2 + i], wrecv.at[2 + i], d) for i, d in enumerate((xp, xm, x2))]
+    L4 = ((k * 4 + z) * 2 + yl) * 4
+    w_src = wo_hbm.at[
+        pl.ds(pl.multiple_of(L4 * 16, 64), 64), pl.ds(pl.multiple_of(peer * 2048, 2048), 2048)
+    ]
+    w0 = [
+        rcopy(w_src, wpeer_v.at[pl.ds(pl.multiple_of(L4 * 16, 64), 64)], wsend.at[i], wrecv.at[i], d)
+        for i, d in enumerate((head_peer, diag))
+    ]
+
+    def w_rows(first, count):
+        return wpeer_v.at[pl.ds(pl.multiple_of(first * 16, 64), count * 16)]
+
     L8 = (k * 4 + z) * 8
-    eight = wpeer_v.at[pl.ds(L8, 8)]
-    w3 = [rcopy(eight, eight, wsend.at[5 + i], wrecv.at[5 + i], d) for i, d in enumerate((zp, zm))]
+    eight = w_rows(L8, 8)
+    own_lo, own_hi = w_rows(L8, 4), w_rows(L8 + 4, 4)
+    w3a = [rcopy(own_lo, own_lo, wsend.at[2], wrecv.at[2], zp), rcopy(own_hi, own_hi, wsend.at[3], wrecv.at[3], zm)]
+    w3b = [rcopy(own_hi, own_hi, wsend.at[10], wrecv.at[10], zp), rcopy(own_lo, own_lo, wsend.at[11], wrecv.at[11], zm)]
     Lm = (k * 4 + (z + 3) % 4) * 8
     Lp = (k * 4 + (z + 1) % 4) * 8
-    lo4 = wpeer_v.at[pl.ds(Lm, 4)]
-    hi4 = wpeer_v.at[pl.ds(Lp + 4, 4)]
-    w4 = [rcopy(lo4, lo4, wsend.at[7], wrecv.at[7], zp), rcopy(hi4, hi4, wsend.at[8], wrecv.at[8], zm)]
-    half = wpeer_v.at[pl.ds(k * 32, 32)]
-    w5 = rcopy(half, half, wsend.at[9], wrecv.at[9], sib)
+    lo4 = w_rows(Lm, 4)
+    hi4 = w_rows(Lp + 4, 4)
+    w4 = [rcopy(lo4, lo4, wsend.at[4], wrecv.at[4], zp), rcopy(hi4, hi4, wsend.at[5], wrecv.at[5], zm)]
+    w5 = []
+    for i in range(4):
+        part = w_rows((k * 4 + (z + (0, 1, 3, 2)[i]) % 4) * 8, 8)
+        w5.append(rcopy(part, part, wsend.at[6 + i], wrecv.at[6 + i], sib))
 
     own_slot = k
     prev_slot = 8 + k
@@ -141,16 +148,16 @@
     def wait_slot(g, s):
         slot_copy(s, s, g, S_PREV, sib, s).wait_recv()
 
-    mid = (x == 1) | (x == 2)
-
     def start_own(g):
-        c_prev(g).start()
-
-        @pl.when(x < 3)
+        @pl.when(r < 7)
+        def _():
+            c_prev(g).start()
+
+        @pl.when((x < 3) | (r == 0))
         def _():
             c_pos(g, own_slot).start()
 
-        @pl.when(x == 0)
+        @pl.when((x == 0) | (r == 0))
         def _():
             c_neg(g, own_slot).start()
 
@@ -159,59 +166,69 @@
             c_d2d(g, 0).start()
 
     def f_prev(g):
-        wait_slot(g, 8 + k)
-
-        @pl.when(x == 3)
-        def _():
-            c_pos(g, prev_slot).start()
-
-        @pl.when(x > 0)
-        def _():
-            c_neg(g, prev_slot).start()
-
-        @pl.when(k == 1)
-        def _():
-            c_d2d(g, 4).start()
+        @pl.when(r > 0)
+        def _():
+            wait_slot(g, 8 + k)
+
+            @pl.when(x == 3)
+            def _():
+                c_pos(g, prev_slot).start()
+
+            @pl.when(x > 0)
+            def _():
+                c_neg(g, prev_slot).start()
+
+            @pl.when(k == 1)
+            def _():
+                c_d2d(g, 4).start()
 
     def f_one(g, early):
         @pl.when((x > 0) if early else (x == 0))
         def _():
             wait_slot(g, 2 + k)
 
-            @pl.when(mid)
+            @pl.when(x < 3)
             def _():
                 c_fpos(g).start()
 
             c_d2d(g, 1).start()
 
-    def f_three(g):
-        wait_slot(g, 6 + k)
-
-        @pl.when(mid)
-        def _():
-            c_fneg(g).start()
-
-        c_d2d(g, 3).start()
+    def f_three(g, which):
+        @pl.when(which)
+        def _():
+            wait_slot(g, 6 + k)
+
+            @pl.when(x == 1)
+            def _():
+                c_fneg(g).start()
+
+            c_d2d(g, 3).start()
 
     def f_two(g):
         wait_slot(g, 4 + k)
         c_d2d(g, 2).start()
 
     def wait_sends(g):
-        c_prev(g).wait_send()
+        @pl.when(r < 7)
+        def _():
+            c_prev(g).wait_send()
+
         c_pos(g, own_slot).wait_send()
         c_neg(g, own_slot).wait_send()
 
-        @pl.when(mid)
+        @pl.when(x < 3)
         def _():
             c_fpos(g).wait_send()
+
+        @pl.when(x == 1)
+        def _():
             c_fneg(g).wait_send()
 
         @pl.when(k == 0)
         def _():
             c_d2d(g, 0).wait_send()
 
-        @pl.when(k == 1)
+        @pl.when((k == 1) & (r > 0))
         def _():
             c_d2d(g, 4).wait_send()
 
@@ -238,9 +255,6 @@
     with scope("rel_rows"):
         lax.fori_loop(0, 8, rel_rows, 0)
     gain = gain_ref[...]
-    with scope("barrier"):
-        pl.semaphore_wait(barrier, 10)
-    w0.start()
 
     def norm_rows(i, c):
         rows = pl.ds(i * 32, 32)
@@ -255,31 +269,31 @@
         with scope("norm"):
             lax.fori_loop(i * 4, i * 4 + 4, norm_rows, 0)
 
-    for g in range(2):
-        with scope("kvwait"):
-            kvcopy(2 * g).wait()
-            kvcopy(2 * g + 1).wait()
-        y = jnp.dot(n_v[...], wkv_v[:, g * 256 : g * 256 + 256], preferred_element_type=F32)
-        kv_v[own_slot, g, :, 0:HD] = y[:, 0:HD].astype(BF16)
-        for c in range(4):
-            kv_v[own_slot, g, c * HD : c * HD + HD, HD : 2 * HD] = (
-                y[c * HD : c * HD + HD, HD : 2 * HD].T.astype(BF16)
-            )
-        start_own(g)
-
-        @pl.when(is_root)
-        def _():
-            sink_v[g] = y[:SROWS, :].astype(BF16)
-
-    @pl.when(is_root)
-    def _():
-        for c in s_x:
-            c.start()
-
-    with scope("w0_wait_recv"):
-        w0.wait_recv()
-    w1.start()
-
+    with scope("barrier"):
+        pl.semaphore_wait(barrier, 11)
+
+    with scope("kvwait"):
+        for i in range(4):
+            kvcopy(i).wait()
+    with scope("kv"):
+        y = jnp.dot(n_v[...], wkv_v[...], preferred_element_type=F32)
+        for g in range(2):
+            yg = y[:, g * 256 : g * 256 + 256]
+            kv_v[own_slot, g, :, 0:HD] = yg[:, 0:HD].astype(BF16)
+            for c in range(4):
+                kv_v[own_slot, g, c * HD : c * HD + HD, HD : 2 * HD] = (
+                    yg[c * HD : c * HD + HD, HD : 2 * HD].T.astype(BF16)
+                )
+            if g == 1:
+
+                @pl.when(is_root)
+                def _():
+                    for e in range(2):
+                        sink_v[e] = y[:SROWS, e * 256 : e * 256 + 256].astype(BF16)
+                    for c in s_x:
+                        c.start()
+
+            start_own(g)
     def q_tile(i):
         qcopy(2 * i).wait()
         qcopy(2 * i + 1).wait()
@@ -293,14 +307,6 @@
     with scope("q0"):
         q_tile(0)
 
-    @pl.when(tier_x)
-    def _():
-        @pl.when(jnp.logical_not(is_root))
-        def _():
-            s_x[0].wait_recv()
-
-        s_y.start()
-
     ones = jnp.ones((VR - HD, T), BF16)
 
     def values_t(slot, g):
@@ -311,9 +317,8 @@
         q = q_v[h]
         w = win_ref[h]
         top = None
-        for b, (d, kk) in enumerate(slots):
-            dist = 2 * d + k - kk
-            keys = kv_v[2 * d + kk, g, :, 0:HD]
+        for b, (dist, place) in enumerate(slots):
+            keys = kv_v[place, g, :, 0:HD]
             s = jnp.dot(jnp.concatenate([keys, keys], axis=1), q, preferred_element_type=F32)
             limit = jnp.where(seq >= dist, w - T * dist, -100000)
             rel = rel_v[...]
@@ -331,9 +336,9 @@
             old = m_v[h, 0:1, :]
             top = jnp.maximum(top, old)
         total = None
-        for b, (d, kk) in enumerate(slots):
+        for b, (_, place) in enumerate(slots):
             p = jnp.exp2(s_ref[b * T : b * T + T, :] - top).astype(BF16)
-            o = jnp.dot(values_t(2 * d + kk, g), p, preferred_element_type=F32)
+            o = jnp.dot(values_t(place, g), p, preferred_element_type=F32)
             total = o if total is None else total + o
         if not first:
             total = total + acc_v[h] * jnp.exp2(old - top)
@@ -353,8 +358,8 @@
 
         lax.fori_loop(0, 2, body, scores(g, base, slots, first, sa_v))
 
-    def c_att(pair):
-        return rcopy(att_v.at[pair], attp_v.at[pair], asend.at[pair], arecv.at[pair], head_peer)
+    def c_att(h):
+        return rcopy(att_v.at[h], attp_v.at[h], asend.at[h], arecv.at[h], head_peer)
 
     def finish_head(g, h):
         ks = sink_v[g, :, 0:HD]
@@ -373,136 +378,176 @@
         o = acc_v[h, 0:HD, :] * scale + jnp.dot(vt, p.astype(BF16), preferred_element_type=F32)
         return (o / total).T.astype(BF16)
 
-    def finish(g):
-        for pair in range(2):
-            for h in range(2):
-                att_v[g * 2 + pair, :, h * HD : h * HD + HD] = finish_head(g, g * 4 + pair * 2 + h)
-            c_att(g * 2 + pair).start()
-
-    special = jnp.where(k == 0, 4, 0)
+    def finish(g, heads=(0, 1, 2, 3)):
+        for i in heads:
+            att_v[g * 4 + i] = finish_head(g, g * 4 + i)
+            c_att(g * 4 + i).start()
+
+    def pair_steps(g, h0, steps):
+        items = [(slots, h0 + i) for slots in steps for i in range(2)]
+        bufs = (sa_v, sb_v)
+        last = None
+        for n, (slots, h) in enumerate(items):
+            top = scores(g, h, slots, False, bufs[n % 2])
+            if last is not None:
+                weigh(*last)
+            last = (g, h, slots, False, bufs[n % 2], top)
+        weigh(*last)
+
+    own = (0, own_slot)
+    special = (jnp.where(k == 0, 8, 1), jnp.where((k == 0) & (r > 0), 8, 0))
+    prev_odd = (7 + k, jnp.where(r == 0, k, 9))
+
+    def slot(d, kk):
+        return (2 * d + k - kk, 2 * d + kk)
+
 
     def wait_special(g):
         @pl.when(k == 1)
         def _():
             wait_slot(g, 0)
 
-        @pl.when(k == 0)
+        @pl.when((k == 0) & (r > 0))
         def _():
             wait_slot(g, 9)
 
     with scope("q1"):
         q_tile(1)
     with scope("own0"):
-        step(0, [(0, k)], first=True)
+        step(0, [own], first=True)
     with scope("f_prev0"):
         f_prev(0)
     with scope("f_one0"):
         f_one(0, True)
-    with scope("w1_wait_recv"):
-        w1.wait_recv()
-    for c in w2:
+    for c in w0:
         c.start()
     with scope("own1"):
-        step(1, [(0, k)], first=True)
-
-    @pl.when(tier_y)
-    def _():
-        @pl.when(yl == 1)
-        def _():
-            s_y.wait_recv()
-
-        for c in s_z:
-            c.start()
-
-    with scope("f_prev1"):
-        f_prev(1)
-    with scope("f_one1"):
-        f_one(1, True)
+        step(1, [own], first=True)
+    with scope("tier_x"):
+
+        @pl.when(tier_x)
+        def _():
+            @pl.when(jnp.logical_not(is_root))
+            def _():
+                s_x[0].wait_recv()
+
+            s_y.start()
+
     with scope("wsp0"):
         wait_special(0)
     with scope("step0sp"):
-        step(0, [(special, 0), (4, 1)])
-    with scope("w2wait"):
-        for c in w2:
-            c.wait_recv()
-    for c in w3:
-        c.start()
+        step(0, [special, prev_odd])
+    with scope("f_prev1"):
+        f_prev(1)
     with scope("f_one0b"):
         f_one(0, False)
     with scope("f_three0"):
-        f_three(0)
+        f_three(0, x >= 0)
+    with scope("f_one1"):
+        f_one(1, True)
     with scope("w0_1"):
         wait_slot(0, 2 + (1 - k))
     with scope("step0_1"):
-        step(0, [(1, 0), (1, 1)])
-
-    @pl.when(tier_z)
-    def _():
-        @pl.when(z > 0)
-        def _():
-            s_z[0].wait_recv()
-
-        s_k.start()
-
-    with scope("f_one1b"):
-        f_one(1, False)
-    with scope("f_three1"):
-        f_three(1)
+        step(0, [slot(1, 0), slot(1, 1)])
+    with scope("tier_y"):
+
+        @pl.when(tier_y)
+        def _():
+            @pl.when(yl == 1)
+            def _():
+                s_y.wait_recv()
+
+            for c in s_z:
+                c.start()
+
+    with scope("f_three1a"):
+        f_three(1, x == 1)
     with scope("w0_3"):
         wait_slot(0, 6 + (1 - k))
     with scope("step0_3"):
-        step(0, [(3, 0), (3, 1)])
+        step(0, [slot(3, 0), slot(3, 1)])
+    with scope("w0wait"):
+        for c in w0:
+            c.wait_recv()
+    for c in w3a + w3b:
+        c.start()
+    w5[0].start()
+    with scope("tier_z"):
+
+        @pl.when(tier_z)
+        def _():
+            @pl.when(z > 0)
+            def _():
+                s_z[0].wait_recv()
+
+            s_k.start()
+
+    with scope("wsp1"):
+        wait_special(1)
+    with scope("step1sp"):
+        step(1, [special, prev_odd])
     with scope("f_two0"):
         f_two(0)
-    with scope("w3wait"):
-        for c in w3:
+    with scope("f_one1b"):
+        f_one(1, False)
+    with scope("w0_2"):
+        wait_slot(0, 4 + (1 - k))
+    with scope("step0_2"):
+        step(0, [slot(2, 0), slot(2, 1)])
+    with scope("tier_k"):
+
+        @pl.when(k == 1)
+        def _():
+            s_k.wait_recv()
+
+    with scope("finish0"):
+        finish(0)
+    with scope("f_three1b"):
+        f_three(1, x != 1)
+    with scope("w3await"):
+        for c in w3a:
             c.wait_recv()
     for c in w4:
         c.start()
-    with scope("w0_2"):
-        wait_slot(0, 4 + (1 - k))
-    with scope("step0_2"):
-        step(0, [(2, 0), (2, 1)])
-
-    @pl.when(k == 1)
-    def _():
-        s_k.wait_recv()
-
-    with scope("finish0"):
-        finish(0)
     with scope("w1_1"):
-        wait_special(1)
         wait_slot(1, 2 + (1 - k))
-    with scope("step1a"):
-        step(1, [(special, 0), (4, 1), (1, 0)])
+        wait_slot(1, 6 + (1 - k))
+    with scope("step1b"):
+        step(1, [slot(1, 0), slot(1, 1), slot(3, 0)])
     with scope("f_two1"):
         f_two(1)
+    with scope("w1_2"):
+        wait_slot(1, 4 + (1 - k))
+    tail = [[slot(3, 1), slot(2, 0), slot(2, 1)]]
+    with scope("pairA"):
+        pair_steps(1, 4, tail)
+    with scope("finishA"):
+        finish(1, (0, 1))
+    with scope("pairB"):
+        pair_steps(1, 6, tail)
+    with scope("finishB"):
+        finish(1, (2, 3))
+    with scope("w3bwait"):
+        for c in w3b:
+            c.wait_recv()
+    w5[1].start()
+    w5[2].start()
     with scope("w4wait"):
         for c in w4:
             c.wait_recv()
-    w5.start()
-    with scope("w1_3"):
-        wait_slot(1, 6 + (1 - k))
-    with scope("step1b"):
-        step(1, [(1, 1), (3, 0), (3, 1)])
-    with scope("w1_2"):
-        wait_slot(1, 4 + (1 - k))
-    with scope("step1c"):
-        step(1, [(2, 0), (2, 1)])
-    with scope("finish1"):
-        finish(1)
-
+    w5[3].start()
     with scope("own_copy_wait"):
         own_copy.wait()
-    with scope("w5_wait_recv"):
-        w5.wait_recv()
     NT_ = 512
+
+    def two_heads(ref, pr):
+        return jnp.concatenate([ref[2 * pr], ref[2 * pr + 1]], axis=1)
 
     def proj_own(n, c):
         cols = pl.ds(pl.multiple_of(n * NT_, NT_), NT_)
         y = None
         for pr in range(4):
-            o = jnp.dot(att_v[pr], wown_v[pr * 256 : pr * 256 + 256, cols], preferred_element_type=F32)
+            o = jnp.dot(two_heads(att_v, pr), wown_v[pr * 256 : pr * 256 + 256, cols], preferred_element_type=F32)
             y = o if y is None else y + o
         o0_v[:, cols] = y.astype(BF16)
         return c
@@ -511,23 +556,27 @@
         lax.fori_loop(0, 4, proj_own, 0)
 
     def wrows(pr, cols):
-        return wpeer_v[pl.ds(pr * 16, 16), :, cols].reshape(256, NT_)
-
+        return wpeer_v[pr * 256 : pr * 256 + 256, cols]
+
+    with scope("w5wait"):
+        for i in range(4):
+            part = w_rows(((1 - k) * 4 + (z + (0, 1, 3, 2)[i]) % 4) * 8, 8)
+            rcopy(part, part, wsend.at[6 + i], wrecv.at[6 + i], sib).wait_recv()
     with scope("att01wait"):
-        for pr in range(2):
-            c_att(pr).wait_recv()
+        for h in range(4):
+            c_att(h).wait_recv()
 
     def proj_first(n, c):
         cols = pl.ds(pl.multiple_of(n * NT_, NT_), NT_)
-        y = jnp.dot(attp_v[0], wrows(0, cols), preferred_element_type=F32)
-        o1_v[:, cols] = y + jnp.dot(attp_v[1], wrows(1, cols), preferred_element_type=F32)
+        y = jnp.dot(two_heads(attp_v, 0), wrows(0, cols), preferred_element_type=F32)
+        o1_v[:, cols] = y + jnp.dot(two_heads(attp_v, 1), wrows(1, cols), preferred_element_type=F32)
         return c
 
     with scope("proj_first"):
         lax.fori_loop(0, 4, proj_first, 0)
     with scope("att23wait"):
-        for pr in range(2, 4):
-            c_att(pr).wait_recv()
+        for h in range(4, 8):
+            c_att(h).wait_recv()
 
     def ocopy(n):
         cols = pl.ds(pl.multiple_of(n * NT_, NT_), NT_)
@@ -535,8 +584,8 @@
 
     def proj_last(n, c):
         cols = pl.ds(pl.multiple_of(n * NT_, NT_), NT_)
-        y = jnp.dot(attp_v[2], wrows(2, cols), preferred_element_type=F32)
-        y = y + jnp.dot(attp_v[3], wrows(3, cols), preferred_element_type=F32)
+        y = jnp.dot(two_heads(attp_v, 2), wrows(2, cols), preferred_element_type=F32)
+        y = y + jnp.dot(two_heads(attp_v, 3), wrows(3, cols), preferred_element_type=F32)
         y = (y + o1_v[:, cols]).astype(BF16).astype(F32)
         base = x_v[:, pl.ds(pl.multiple_of(j * 2048 + n * NT_, NT_), NT_)].astype(F32)
         out_v[:, cols] = (base + (o0_v[:, cols].astype(F32) + y)).astype(BF16)
@@ -548,11 +597,8 @@
 
     for g in range(2):
         wait_sends(g)
-    w0.wait_send()
-    w1.wait_send()
-    for c in w2 + w3 + w4:
+    for c in w0 + w3a + w3b + w4 + w5:
         c.wait_send()
-    w5.wait_send()
 
     @pl.when(is_root)
     def _():
@@ -572,8 +618,8 @@
     def _():
         s_k.wait_send()
 
-    for pr in range(4):
-        c_att(pr).wait_send()
+    for h in range(8):
+        c_att(h).wait_send()
     for n in range(4):
         ocopy(n).wait()
 
@@ -594,7 +640,7 @@
             pltpu.VMEM((D, 1024), BF16),
             pltpu.VMEM((D, 512), BF16),
             pltpu.VMEM((1024, 2048), BF16),
-            pltpu.VMEM((64, 16, 2048), BF16),
+            pltpu.VMEM((1024, 2048), BF16),
             pltpu.VMEM((10, 2, T, 256), BF16),
             pltpu.VMEM((2, SROWS, 256), BF16),
             pltpu.VMEM((8, 256, T), BF16),
@@ -603,20 +649,20 @@
             pltpu.VMEM((T, T), jnp.int32),
             pltpu.VMEM((3 * T, T), F32),
             pltpu.VMEM((3 * T, T), F32),
-            pltpu.VMEM((4, T, 256), BF16),
-            pltpu.VMEM((4, T, 256), BF16),
+            pltpu.VMEM((8, T, HD), BF16),
+            pltpu.VMEM((8, T, HD), BF16),
             pltpu.VMEM((T, 2048), BF16),
             pltpu.VMEM((T, 2048), F32),
             pltpu.VMEM((T, 2048), BF16),
             dma((13,)),
             dma((2, N_HALO_SEND)),
             dma((2, 10)),
-            dma((10,)),
-            dma((10,)),
+            dma((12,)),
+            dma((12,)),
             dma((8,)),
             dma((4,)),
-            dma((4,)),
-            dma((4,)),
+            dma((8,)),
+            dma((8,)),
             dma((4,)),
         ],
         compiler_params=pltpu.CompilerParams(

time: 91.1 us -> 74.3 us (0.82)
  the two profiles are of different devices: /device:TPU:1 before, /device:TPU:96 now
where the time goes in v3:
time: 74.3 us; the launch traced here: 73.6 us
  Pallas kernels  70.5 us (95%)
  local copies, waits for them, and re-layouts  3.16 us (4%)
    pallas_call x1, Pallas kernels, local(): pl.pallas_call(kernel, out_shape=jax.ShapeDtypeStruct((T, 2048), BF16), i...  70.5 us
    unnamed x1, local copies, waits for them, and re-layouts  3.16 us

profile of v3, /device:TPU:96, one launch (start us, length us, event | category | flops | bytes accessed | tf_op | source)
XLA Modules:
  0.0 73.6 jit_solution(3865930649093912533)
XLA Ops:
  0.0 70.5 %block.1 = bf16[512,2048]{1,0:T(8,128)(2,1)} custom-call(bf16[512,4096]{1,0:T(8,128)(2,1)} %x_hbm.1, f32[1,4096]{1,0:T(1,128)} %bitcast.1, bf16[4096,1024]{1,0:T(8,128)(2,1)} %wq_hbm.1, bf16[4096,256]{1,0:T(8,128)(2,1)} %wk_hbm.1, bf16[4096,256]{1,0:T(8,128)(2,1)} %wv_hbm.1, bf16[1024,4096]{1,0:T(8,128)(2,1)} %wo_hbm.1, s32[8]{0:T(128)} %win_ref.1, ...), custom_call_target="tpu_custom_call" | custom-call | tf_op jit(solution)/shard_map/block/pallas_call | solution.py:632
  70.5 3.2 %copy.11 = bf16[512,2048]{1,0:T(8,128)(2,1)} copy(bf16[512,2048]{1,0:T(8,128)(2,1)} %block.1) | data formatting | bytes 4194304

commit v4 on v3

--- a/solution.py
+++ b/solution.py
@@ -165,8 +165,8 @@
         def _():
             c_d2d(g, 0).start()
 
-    def f_prev(g):
-        @pl.when(r > 0)
+    def f_prev(g, which):
+        @pl.when((r > 0) & which)
         def _():
             wait_slot(g, 8 + k)
 
@@ -416,7 +416,7 @@
     with scope("own0"):
         step(0, [own], first=True)
     with scope("f_prev0"):
-        f_prev(0)
+        f_prev(0, x >= 0)
     with scope("f_one0"):
         f_one(0, True)
     for c in w0:
@@ -438,40 +438,50 @@
     with scope("step0sp"):
         step(0, [special, prev_odd])
     with scope("f_prev1"):
-        f_prev(1)
+        f_prev(1, x != 1)
+    with scope("f_three0a"):
+        f_three(0, x == 1)
+    with scope("f_prev1b"):
+        f_prev(1, x == 1)
+    with scope("wsp1"):
+        wait_special(1)
+    with scope("step1sp"):
+        step(1, [special, prev_odd])
     with scope("f_one0b"):
         f_one(0, False)
     with scope("f_three0"):
-        f_three(0, x >= 0)
+        f_three(0, x != 1)
     with scope("f_one1"):
         f_one(1, True)
+    with scope("f_three1a"):
+        f_three(1, x == 1)
+    with scope("tier_y"):
+
+        @pl.when(tier_y)
+        def _():
+            @pl.when(yl == 1)
+            def _():
+                s_y.wait_recv()
+
+            for c in s_z:
+                c.start()
+
     with scope("w0_1"):
         wait_slot(0, 2 + (1 - k))
     with scope("step0_1"):
         step(0, [slot(1, 0), slot(1, 1)])
-    with scope("tier_y"):
-
-        @pl.when(tier_y)
-        def _():
-            @pl.when(yl == 1)
-            def _():
-                s_y.wait_recv()
-
-            for c in s_z:
-                c.start()
-
-    with scope("f_three1a"):
-        f_three(1, x == 1)
-    with scope("w0_3"):
-        wait_slot(0, 6 + (1 - k))
-    with scope("step0_3"):
-        step(0, [slot(3, 0), slot(3, 1)])
     with scope("w0wait"):
         for c in w0:
             c.wait_recv()
     for c in w3a + w3b:
         c.start()
     w5[0].start()
+    with scope("f_one1b"):
+        f_one(1, False)
+    with scope("w0_3"):
+        wait_slot(0, 6 + (1 - k))
+    with scope("step0_3"):
+        step(0, [slot(3, 0), slot(3, 1)])
     with scope("tier_z"):
 
         @pl.when(tier_z)
@@ -482,33 +492,27 @@
 
             s_k.start()
 
-    with scope("wsp1"):
-        wait_special(1)
-    with scope("step1sp"):
-        step(1, [special, prev_odd])
     with scope("f_two0"):
         f_two(0)
-    with scope("f_one1b"):
-        f_one(1, False)
     with scope("w0_2"):
         wait_slot(0, 4 + (1 - k))
-    with scope("step0_2"):
-        step(0, [slot(2, 0), slot(2, 1)])
+    last0 = [[slot(2, 0), slot(2, 1)]]
+    with scope("pair0A"):
+        pair_steps(0, 0, last0)
     with scope("tier_k"):
 
         @pl.when(k == 1)
         def _():
             s_k.wait_recv()
 
-    with scope("finish0"):
-        finish(0)
+    with scope("finish0A"):
+        finish(0, (0, 1))
+    with scope("pair0B"):
+        pair_steps(0, 2, last0)
+    with scope("finish0B"):
+        finish(0, (2, 3))
     with scope("f_three1b"):
         f_three(1, x != 1)
-    with scope("w3await"):
-        for c in w3a:
-            c.wait_recv()
-    for c in w4:
-        c.start()
     with scope("w1_1"):
         wait_slot(1, 2 + (1 - k))
         wait_slot(1, 6 + (1 - k))
@@ -516,6 +520,11 @@
         step(1, [slot(1, 0), slot(1, 1), slot(3, 0)])
     with scope("f_two1"):
         f_two(1)
+    with scope("w3await"):
+        for c in w3a:
+            c.wait_recv()
+    for c in w4:
+        c.start()
     with scope("w1_2"):
         wait_slot(1, 4 + (1 - k))
     tail = [[slot(3, 1), slot(2, 0), slot(2, 1)]]

time: 74.3 us -> 70.7 us (0.952)
  Pallas kernels: 70.5 us -> 67.1 us
    pallas_call x1, Pallas kernels: 70.5 us -> 67.1 us  [local(): pl.pallas_call(kernel, out_shape=jax.ShapeDtypeStruct((T, 2048), BF16), i...]
where the time goes in v4:
time: 70.7 us; the launch traced here: 70.2 us
  Pallas kernels  67.1 us (95%)
  local copies, waits for them, and re-layouts  3.16 us (4%)
    pallas_call x1, Pallas kernels, local(): pl.pallas_call(kernel, out_shape=jax.ShapeDtypeStruct((T, 2048), BF16), i...  67.1 us
    unnamed x1, local copies, waits for them, and re-layouts  3.16 us

profile of v4, /device:TPU:96, one launch (start us, length us, event | category | flops | bytes accessed | tf_op | source)
XLA Modules:
  0.0 70.2 jit_solution(18361711049656113951)
XLA Ops:
  0.0 67.1 %block.1 = bf16[512,2048]{1,0:T(8,128)(2,1)} custom-call(bf16[512,4096]{1,0:T(8,128)(2,1)} %x_hbm.1, f32[1,4096]{1,0:T(1,128)} %bitcast.1, bf16[4096,1024]{1,0:T(8,128)(2,1)} %wq_hbm.1, bf16[4096,256]{1,0:T(8,128)(2,1)} %wk_hbm.1, bf16[4096,256]{1,0:T(8,128)(2,1)} %wv_hbm.1, bf16[1024,4096]{1,0:T(8,128)(2,1)} %wo_hbm.1, s32[8]{0:T(128)} %win_ref.1, ...), custom_call_target="tpu_custom_call" | custom-call | tf_op jit(solution)/shard_map/block/pallas_call | solution.py:641
  67.1 3.2 %copy.11 = bf16[512,2048]{1,0:T(8,128)(2,1)} copy(bf16[512,2048]{1,0:T(8,128)(2,1)} %block.1) | data formatting | bytes 4194304

commit v5 on v4

--- a/solution.py
+++ b/solution.py
@@ -345,10 +345,16 @@
         acc_v[h] = total
         m_v[h] = jnp.broadcast_to(top, (8, T))
 
-    def step(g, slots, first=False):
+    def step(g, slots, first=False, halfway=None):
         base = g * 4
 
         def body(i, top):
+            if halfway is not None:
+
+                @pl.when(i == 1)
+                def _():
+                    halfway()
+
             h = base + 2 * i
             top_b = scores(g, h + 1, slots, first, sb_v)
             weigh(g, h, slots, first, sa_v, top)
@@ -453,8 +459,6 @@
         f_three(0, x != 1)
     with scope("f_one1"):
         f_one(1, True)
-    with scope("f_three1a"):
-        f_three(1, x == 1)
     with scope("tier_y"):
 
         @pl.when(tier_y)
@@ -470,6 +474,8 @@
         wait_slot(0, 2 + (1 - k))
     with scope("step0_1"):
         step(0, [slot(1, 0), slot(1, 1)])
+    with scope("f_three1a"):
+        f_three(1, x == 1)
     with scope("w0wait"):
         for c in w0:
             c.wait_recv()
@@ -481,7 +487,7 @@
     with scope("w0_3"):
         wait_slot(0, 6 + (1 - k))
     with scope("step0_3"):
-        step(0, [slot(3, 0), slot(3, 1)])
+        step(0, [slot(3, 0), slot(3, 1)], halfway=lambda: f_two(0))
     with scope("tier_z"):
 
         @pl.when(tier_z)
@@ -492,8 +498,6 @@
 
             s_k.start()
 
-    with scope("f_two0"):
-        f_two(0)
     with scope("w0_2"):
         wait_slot(0, 4 + (1 - k))
     last0 = [[slot(2, 0), slot(2, 1)]]
@@ -517,9 +521,7 @@
         wait_slot(1, 2 + (1 - k))
         wait_slot(1, 6 + (1 - k))
     with scope("step1b"):
-        step(1, [slot(1, 0), slot(1, 1), slot(3, 0)])
-    with scope("f_two1"):
-        f_two(1)
+        step(1, [slot(1, 0), slot(1, 1), slot(3, 0)], halfway=lambda: f_two(1))
     with scope("w3await"):
         for c in w3a:
             c.wait_recv()
@@ -558,7 +560,8 @@
         for pr in range(4):
             o = jnp.dot(two_heads(att_v, pr), wown_v[pr * 256 : pr * 256 + 256, cols], preferred_element_type=F32)
             y = o if y is None else y + o
-        o0_v[:, cols] = y.astype(BF16)
+        base = x_v[:, pl.ds(pl.multiple_of(j * 2048 + n * NT_, NT_), NT_)].astype(F32)
+        o0_v[:, cols] = base + y.astype(BF16).astype(F32)
         return c
 
     with scope("proj_own"):
@@ -583,8 +586,20 @@
 
     with scope("proj_first"):
         lax.fori_loop(0, 4, proj_first, 0)
-    with scope("att23wait"):
-        for h in range(4, 8):
+    with scope("att45wait"):
+        for h in range(4, 6):
+            c_att(h).wait_recv()
+
+    def proj_mid(n, c):
+        cols = pl.ds(pl.multiple_of(n * NT_, NT_), NT_)
+        y = jnp.dot(two_heads(attp_v, 2), wrows(2, cols), preferred_element_type=F32)
+        o1_v[:, cols] = o1_v[:, cols] + y
+        return c
+
+    with scope("proj_mid"):
+        lax.fori_loop(0, 4, proj_mid, 0)
+    with scope("att67wait"):
+        for h in range(6, 8):
             c_att(h).wait_recv()
 
     def ocopy(n):
@@ -593,11 +608,9 @@
 
     def proj_last(n, c):
         cols = pl.ds(pl.multiple_of(n * NT_, NT_), NT_)
-        y = jnp.dot(two_heads(attp_v, 2), wrows(2, cols), preferred_element_type=F32)
-        y = y + jnp.dot(two_heads(attp_v, 3), wrows(3, cols), preferred_element_type=F32)
+        y = jnp.dot(two_heads(attp_v, 3), wrows(3, cols), preferred_element_type=F32)
         y = (y + o1_v[:, cols]).astype(BF16).astype(F32)
-        base = x_v[:, pl.ds(pl.multiple_of(j * 2048 + n * NT_, NT_), NT_)].astype(F32)
-        out_v[:, cols] = (base + (o0_v[:, cols].astype(F32) + y)).astype(BF16)
+        out_v[:, cols] = (o0_v[:, cols] + y).astype(BF16)
         ocopy(n).start()
         return c
 
@@ -660,7 +673,7 @@
             pltpu.VMEM((3 * T, T), F32),
             pltpu.VMEM((8, T, HD), BF16),
             pltpu.VMEM((8, T, HD), BF16),
-            pltpu.VMEM((T, 2048), BF16),
+            pltpu.VMEM((T, 2048), F32),
             pltpu.VMEM((T, 2048), F32),
             pltpu.VMEM((T, 2048), BF16),
             dma((13,)),

time: 70.7 us -> 67.4 us (0.953)
  Pallas kernels: 67.1 us -> 64 us
    pallas_call x1, Pallas kernels: 67.1 us -> 64 us  [local(): pl.pallas_call(kernel, out_shape=jax.ShapeDtypeStruct((T, 2048), BF16), i...]
where the time goes in v5:
time: 67.4 us; the launch traced here: 67.2 us
  Pallas kernels  64 us (95%)
  local copies, waits for them, and re-layouts  3.16 us (5%)
    pallas_call x1, Pallas kernels, local(): pl.pallas_call(kernel, out_shape=jax.ShapeDtypeStruct((T, 2048), BF16), i...  64 us
    unnamed x1, local copies, waits for them, and re-layouts  3.16 us

profile of v5, /device:TPU:96, one launch (start us, length us, event | category | flops | bytes accessed | tf_op | source)
XLA Modules:
  0.0 67.2 jit_solution(414870102500688614)
XLA Ops:
  0.0 64.0 %block.1 = bf16[512,2048]{1,0:T(8,128)(2,1)} custom-call(bf16[512,4096]{1,0:T(8,128)(2,1)} %x_hbm.1, f32[1,4096]{1,0:T(1,128)} %bitcast.1, bf16[4096,1024]{1,0:T(8,128)(2,1)} %wq_hbm.1, bf16[4096,256]{1,0:T(8,128)(2,1)} %wk_hbm.1, bf16[4096,256]{1,0:T(8,128)(2,1)} %wv_hbm.1, bf16[1024,4096]{1,0:T(8,128)(2,1)} %wo_hbm.1, s32[8]{0:T(128)} %win_ref.1, ...), custom_call_target="tpu_custom_call" | custom-call | tf_op jit(solution)/shard_map/block/pallas_call | solution.py:654
  64.0 3.2 %copy.11 = bf16[512,2048]{1,0:T(8,128)(2,1)} copy(bf16[512,2048]{1,0:T(8,128)(2,1)} %block.1) | data formatting | bytes 4194304
